TPU v7x, 32 devices: a 4x4x1 block of a 4x4x8 slice. The times are simulated.
32 devices in a mesh: dp: 1 (over z), sp: 4 (over y), cp: 8 (over x, core).
Axes of the slice: x: 4, y: 4, z: 1, core: 2. Of those that a mesh axis runs over, the one named last changes fastest.
The devices are a block of a 4x4x8 slice.
Arguments:
- hidden: bfloat16 [8, 4096, 3072], P('dp', ('cp', 'sp'))
- seg_ids: int32 [8, 4096], P('dp', ('cp', 'sp'))
- w_qkv: bfloat16 [3072, 3, 24, 128], replicated
- w_out: bfloat16 [24, 128, 3072], replicated
Outputs:
- output: bfloat16 [8, 4096, 3072], P('dp', ('cp', 'sp'))
All inputs are finite; a program needn't handle non-finite values.
Results may differ from a plain program's by a relative error of at most 0.00599118.
Values are sent between devices in bfloat16 or wider.
A program may use at most 768 MiB of HBM per device.

v0:
```python
import jax
import jax.numpy as jnp
from jax import lax
from jax.sharding import PartitionSpec as P

MASK_VALUE = -1e30


def solution(mesh):
    cp_size = mesh.shape['cp']
    shift_pairs = [(source, (source + 1) % cp_size) for source in range(cp_size)]
    token_spec = P('dp', ('cp', 'sp'), None)
    seg_spec = P('dp', ('cp', 'sp'))

    def local_layer(hidden, seg_ids, w_qkv, w_out):
        batch_size, tokens, model_dim = hidden.shape
        num_heads, head_dim = w_out.shape[0], w_out.shape[1]
        logit_scale = head_dim ** -0.5
        projected = jnp.dot(hidden, w_qkv.reshape(model_dim, 3 * num_heads * head_dim), preferred_element_type=jnp.float32)
        projected = projected.astype(jnp.bfloat16).reshape(batch_size, tokens, 3, num_heads, head_dim)
        projected = lax.all_to_all(projected, 'sp', 3, 1, tiled=True)
        seg_query = lax.all_gather(seg_ids, 'sp', axis=1, tiled=True)
        queries = projected[:, :, 0]
        kv_local = projected[:, :, 1:]
        block_len = queries.shape[1]
        local_heads = queries.shape[2]

        def absorb(running, kv_blk, seg_blk):
            run_max, run_sum, accum_out = running
            scores = jnp.einsum('bqhd,bkhd->bhqk', queries, kv_blk[:, :, 0], preferred_element_type=jnp.float32) * logit_scale
            allowed = seg_query[:, None, :, None] == seg_blk[:, None, None, :]
            scores = jnp.where(allowed, scores, MASK_VALUE)
            new_max = jnp.maximum(run_max, jnp.max(scores, axis=-1))
            weights = jnp.where(allowed, jnp.exp(scores - new_max[..., None]), 0.0)
            rescale = jnp.exp(run_max - new_max)
            run_sum = run_sum * rescale + jnp.sum(weights, axis=-1)
            accum_out = accum_out * rescale[..., None] + jnp.einsum('bhqk,bkhd->bhqd', weights.astype(jnp.bfloat16), kv_blk[:, :, 1], preferred_element_type=jnp.float32)
            return new_max, run_sum, accum_out

        stat_shape = (batch_size, local_heads, block_len)
        start_state = (jnp.full(stat_shape, MASK_VALUE, jnp.float32), jnp.zeros(stat_shape, jnp.float32), jnp.zeros(stat_shape + (head_dim,), jnp.float32))
        running = absorb(start_state, kv_local, seg_query)

        def pass_step(step_idx, loop_state):
            running, kv_cur, seg_cur = loop_state
            kv_cur = lax.ppermute(kv_cur, 'cp', shift_pairs)
            seg_cur = lax.ppermute(seg_cur, 'cp', shift_pairs)
            return absorb(running, kv_cur, seg_cur), kv_cur, seg_cur

        running = lax.fori_loop(1, cp_size, pass_step, (running, kv_local, seg_query))[0]
        run_max, run_sum, accum_out = running
        attn_out = (accum_out / run_sum[..., None]).astype(jnp.bfloat16)
        attn_out = lax.all_to_all(attn_out, 'sp', 2, 1, tiled=True)
        result = jnp.einsum('bhnd,hdc->bnc', attn_out, w_out, preferred_element_type=jnp.float32)
        return result.astype(jnp.bfloat16)

    return jax.shard_map(local_layer, mesh=mesh, in_specs=(token_spec, seg_spec, P(), P()), out_specs=token_spec, check_vma=False)
```

profile of v0, /device:TPU:99, one launch (start us, length us, event | category | flops | bytes accessed | tf_op | source)
XLA Modules:
  0.0 2164.8 jit_solution(11408137852507358586)
XLA Ops:
  0.0 77.0 %reshape.34 = bf16[3072,9216,1]{1,0,2:T(8,128)(2,1)} reshape(bf16[3072,3,24,128]{3,2,1,0:T(8,128)(2,1)} %param.8) | data formatting | bytes 113246208 | tf_op jit(solution)/shard_map/reshape | solution.py:19
  77.0 64.6 %convolution_convert_fusion = bf16[8,128,9216]{2,1,0:T(8,128)(2,1)S(1)} fusion(bf16[8,128,3072]{2,1,0:T(8,128)(2,1)} %param.6, bf16[3072,9216,1]{1,0,2:T(8,128)(2,1)} %reshape.34), kind=kOutput, calls=%fused_computation.26 | convolution fusion | flops 57991495680 | bytes 81788928 | tf_op jit(solution)/shard_map/dot_general | solution.py:19
  161.1 210.2 %all_gather.3 = s32[8,512]{1,0:T(8,128)S(1)} all-gather(s32[8,128]{1,0:T(8,128)S(1)} %copy-done.2), channel_id=1, replica_groups=mesh['dp'=1,'sp'=4,'cp'=8] {'sp'}, dimensions={1}, use_global_device_ids=true | all-gather | bytes 20480 | tf_op jit(solution)/shard_map/all_gather | solution.py:22
  396.1 22.9 %fusion.12 = (f32[8,6,512]{2,1,0:T(8,128)S(1)}, f32[8,6,512,512]{2,3,1,0:T(8,128)}) fusion(pred[8,512,512]{1,2,0:T(8,128)(4,1)} %broadcast_compare_fusion.1, bf16[8,512,3,6,128]{4,1,3,0,2:T(8,128)(2,1)} %bitcast.60), kind=kOutput, calls=%fused_computation.19 | convolution fusion | flops 3258949632 | bytes 65110016 | tf_op jit(solution)/shard_map/bqhd,bkhd->bhqk/dot_general | solution.py:30
  419.0 22.0 %fusion.14 = f32[8,6,512]{2,1,0:T(8,128)S(1)} fusion(f32[8,6,512,512]{2,3,1,0:T(8,128)} %get-tuple-element.73, f32[8,6,512]{2,1,0:T(8,128)S(1)} %broadcast_maximum_fusion, pred[8,512,512]{1,2,0:T(8,128)(4,1)S(1)} %copy-done.1), kind=kLoop, calls=%fused_computation.21 | loop fusion | flops 62889984 | bytes 52625408 | tf_op jit(solution)/shard_map/reduce_sum | solution.py:36
  441.1 27.9 %broadcast_add_fusion = f32[8,6,512,128]{3,2,1,0:T(8,128)} fusion(f32[8,6,512]{2,1,0:T(8,128)S(1)} %get-tuple-element.70, bf16[8,512,3,6,128]{4,1,3,0,2:T(8,128)(2,1)} %bitcast.61, f32[8,6,512,512]{2,3,1,0:T(8,128)} %get-tuple-element.73, f32[8,6,512]{2,1,0:T(8,128)S(1)} %broadcast_maximum_fusion, pred[8,512,512]{1,2,0:T(8,128)(4,1)S(1)} %copy-done.1), kind=kOutput, calls=%fused_computation.34 | convolution fusion | flops 3287285760 | bytes 71499776 | tf_op jit(solution)/shard_map/bhqk,bkhd->bhqd/dot_general | solution.py:37
  469.1 1584.6 %while.18 = (s32[]{:T(128)}, f32[8,6,512]{2,1,0:T(8,128)S(1)}, f32[8,6,512]{2,1,0:T(8,128)S(1)}, f32[8,6,512,128]{3,2,1,0:T(8,128)}, bf16[8,512,2,6,128]{4,1,3,0...) while((s32[]{:T(128)}, f32[8,6,512]{2,1,0:T(8,128)S(1)}, ...), condition=%wide.region_5.6_spmd, body=%wide.region_2.5_spmd.sunk | while | flops 6614466560 | bytes 280625312 | solution.py:50
  474.7 135.5 %collective-permute-done = s32[8,512]{1,0:T(8,128)S(1)} collective-permute-done((s32[8,512]{1,0:T(8,128)S(1)}, s32[8,512]{1,0:T(8,128)S(1)}, u32[]{:S(2)}, u32[]{:S(2)}) %collective-permute-start) | collective-permute-done | bytes 16416 | tf_op jit(solution)/shard_map/while/body/eval_jaxpr/ppermute | solution.py:47
  611.6 22.3 %fusion.40 = (f32[8,6,512]{2,1,0:T(8,128)S(1)}, f32[8,6,512,512]{2,3,1,0:T(8,128)}) fusion(pred[8,512,512]{1,2,0:T(8,128)(4,1)S(1)} %broadcast_compare_fusion.3, bf16[8,512,6,128]{3,1,2,0:T(8,128)(2,1)} %get-tuple-element.156, bf16[8,512,2,6,128]{4,1,3,0,2:T(8,128)(2,1)} %collective-permute-done.1), kind=kOutput, calls=%fused_computation.2.clone.1 | convolution fusion | flops 3258949632 | bytes 65110016 | tf_op jit(solution)/shard_map/while/body/eval_jaxpr/bqhd,bkhd->bhqk/dot_general | solution.py:30
  633.9 22.0 %fusion.41 = f32[8,6,512]{2,1,0:T(8,128)S(1)} fusion(f32[8,6,512,512]{2,3,1,0:T(8,128)} %get-tuple-element.128, f32[8,6,512]{2,1,0:T(8,128)S(1)} %max.4, pred[8,512,512]{1,2,0:T(8,128)(4,1)S(1)} %broadcast_compare_fusion.3), kind=kLoop, calls=%fused_computation.4.clone.1 | loop fusion | flops 62889984 | bytes 52625408 | tf_op jit(solution)/shard_map/while/body/eval_jaxpr/reduce_sum | solution.py:36
  667.3 30.7 %multiply_add_fusion.5 = f32[8,6,512,128]{3,2,1,0:T(8,128)} fusion(f32[8,6,512,128]{3,2,1,0:T(8,128)} %get-tuple-element.143, f32[8,6,512]{2,1,0:T(8,128)S(1)} %get-tuple-element.130, bf16[8,512,2,6,128]{4,1,3,0,2:T(8,128)(2,1)} %collective-permute-done.1, f32[8,6,512,512]{2,3,1,0:T(8,128)} %get-tuple-element.128, f32[8,6,512]{2,1,0:T(8,128)S(1)} %max.4, ...), kind=kOutput, calls=%fused_computation.7.clone.1 | convolution fusion | flops 3290431488 | bytes 84082688 | tf_op jit(solution)/shard_map/while/body/eval_jaxpr/bhqk,bkhd->bhqd/dot_general | solution.py:37
  700.6 135.5 %collective-permute-done = s32[8,512]{1,0:T(8,128)S(1)} collective-permute-done((s32[8,512]{1,0:T(8,128)S(1)}, s32[8,512]{1,0:T(8,128)S(1)}, u32[]{:S(2)}, u32[]{:S(2)}) %collective-permute-start) | collective-permute-done | bytes 16416 | tf_op jit(solution)/shard_map/while/body/eval_jaxpr/ppermute | solution.py:47
  837.5 22.3 %fusion.40 = (f32[8,6,512]{2,1,0:T(8,128)S(1)}, f32[8,6,512,512]{2,3,1,0:T(8,128)}) fusion(pred[8,512,512]{1,2,0:T(8,128)(4,1)S(1)} %broadcast_compare_fusion.3, bf16[8,512,6,128]{3,1,2,0:T(8,128)(2,1)} %get-tuple-element.156, bf16[8,512,2,6,128]{4,1,3,0,2:T(8,128)(2,1)} %collective-permute-done.1), kind=kOutput, calls=%fused_computation.2.clone.1 | convolution fusion | flops 3258949632 | bytes 65110016 | tf_op jit(solution)/shard_map/while/body/eval_jaxpr/bqhd,bkhd->bhqk/dot_general | solution.py:30
  893.3 30.7 %multiply_add_fusion.5 = f32[8,6,512,128]{3,2,1,0:T(8,128)} fusion(f32[8,6,512,128]{3,2,1,0:T(8,128)} %get-tuple-element.143, f32[8,6,512]{2,1,0:T(8,128)S(1)} %get-tuple-element.130, bf16[8,512,2,6,128]{4,1,3,0,2:T(8,128)(2,1)} %collective-permute-done.1, f32[8,6,512,512]{2,3,1,0:T(8,128)} %get-tuple-element.128, f32[8,6,512]{2,1,0:T(8,128)S(1)} %max.4, ...), kind=kOutput, calls=%fused_computation.7.clone.1 | convolution fusion | flops 3290431488 | bytes 84082688 | tf_op jit(solution)/shard_map/while/body/eval_jaxpr/bhqk,bkhd->bhqd/dot_general | solution.py:37
  926.5 135.5 %collective-permute-done = s32[8,512]{1,0:T(8,128)S(1)} collective-permute-done((s32[8,512]{1,0:T(8,128)S(1)}, s32[8,512]{1,0:T(8,128)S(1)}, u32[]{:S(2)}, u32[]{:S(2)}) %collective-permute-start) | collective-permute-done | bytes 16416 | tf_op jit(solution)/shard_map/while/body/eval_jaxpr/ppermute | solution.py:47
  1063.5 22.3 %fusion.40 = (f32[8,6,512]{2,1,0:T(8,128)S(1)}, f32[8,6,512,512]{2,3,1,0:T(8,128)}) fusion(pred[8,512,512]{1,2,0:T(8,128)(4,1)S(1)} %broadcast_compare_fusion.3, bf16[8,512,6,128]{3,1,2,0:T(8,128)(2,1)} %get-tuple-element.156, bf16[8,512,2,6,128]{4,1,3,0,2:T(8,128)(2,1)} %collective-permute-done.1), kind=kOutput, calls=%fused_computation.2.clone.1 | convolution fusion | flops 3258949632 | bytes 65110016 | tf_op jit(solution)/shard_map/while/body/eval_jaxpr/bqhd,bkhd->bhqk/dot_general | solution.py:30
  1119.2 30.7 %multiply_add_fusion.5 = f32[8,6,512,128]{3,2,1,0:T(8,128)} fusion(f32[8,6,512,128]{3,2,1,0:T(8,128)} %get-tuple-element.143, f32[8,6,512]{2,1,0:T(8,128)S(1)} %get-tuple-element.130, bf16[8,512,2,6,128]{4,1,3,0,2:T(8,128)(2,1)} %collective-permute-done.1, f32[8,6,512,512]{2,3,1,0:T(8,128)} %get-tuple-element.128, f32[8,6,512]{2,1,0:T(8,128)S(1)} %max.4, ...), kind=kOutput, calls=%fused_computation.7.clone.1 | convolution fusion | flops 3290431488 | bytes 84082688 | tf_op jit(solution)/shard_map/while/body/eval_jaxpr/bhqk,bkhd->bhqd/dot_general | solution.py:37
  1152.5 135.5 %collective-permute-done = s32[8,512]{1,0:T(8,128)S(1)} collective-permute-done((s32[8,512]{1,0:T(8,128)S(1)}, s32[8,512]{1,0:T(8,128)S(1)}, u32[]{:S(2)}, u32[]{:S(2)}) %collective-permute-start) | collective-permute-done | bytes 16416 | tf_op jit(solution)/shard_map/while/body/eval_jaxpr/ppermute | solution.py:47
  1289.4 22.3 %fusion.40 = (f32[8,6,512]{2,1,0:T(8,128)S(1)}, f32[8,6,512,512]{2,3,1,0:T(8,128)}) fusion(pred[8,512,512]{1,2,0:T(8,128)(4,1)S(1)} %broadcast_compare_fusion.3, bf16[8,512,6,128]{3,1,2,0:T(8,128)(2,1)} %get-tuple-element.156, bf16[8,512,2,6,128]{4,1,3,0,2:T(8,128)(2,1)} %collective-permute-done.1), kind=kOutput, calls=%fused_computation.2.clone.1 | convolution fusion | flops 3258949632 | bytes 65110016 | tf_op jit(solution)/shard_map/while/body/eval_jaxpr/bqhd,bkhd->bhqk/dot_general | solution.py:30
  1345.1 30.7 %multiply_add_fusion.5 = f32[8,6,512,128]{3,2,1,0:T(8,128)} fusion(f32[8,6,512,128]{3,2,1,0:T(8,128)} %get-tuple-element.143, f32[8,6,512]{2,1,0:T(8,128)S(1)} %get-tuple-element.130, bf16[8,512,2,6,128]{4,1,3,0,2:T(8,128)(2,1)} %collective-permute-done.1, f32[8,6,512,512]{2,3,1,0:T(8,128)} %get-tuple-element.128, f32[8,6,512]{2,1,0:T(8,128)S(1)} %max.4, ...), kind=kOutput, calls=%fused_computation.7.clone.1 | convolution fusion | flops 3290431488 | bytes 84082688 | tf_op jit(solution)/shard_map/while/body/eval_jaxpr/bhqk,bkhd->bhqd/dot_general | solution.py:37
  1378.4 135.5 %collective-permute-done = s32[8,512]{1,0:T(8,128)S(1)} collective-permute-done((s32[8,512]{1,0:T(8,128)S(1)}, s32[8,512]{1,0:T(8,128)S(1)}, u32[]{:S(2)}, u32[]{:S(2)}) %collective-permute-start) | collective-permute-done | bytes 16416 | tf_op jit(solution)/shard_map/while/body/eval_jaxpr/ppermute | solution.py:47
  1515.3 22.3 %fusion.40 = (f32[8,6,512]{2,1,0:T(8,128)S(1)}, f32[8,6,512,512]{2,3,1,0:T(8,128)}) fusion(pred[8,512,512]{1,2,0:T(8,128)(4,1)S(1)} %broadcast_compare_fusion.3, bf16[8,512,6,128]{3,1,2,0:T(8,128)(2,1)} %get-tuple-element.156, bf16[8,512,2,6,128]{4,1,3,0,2:T(8,128)(2,1)} %collective-permute-done.1), kind=kOutput, calls=%fused_computation.2.clone.1 | convolution fusion | flops 3258949632 | bytes 65110016 | tf_op jit(solution)/shard_map/while/body/eval_jaxpr/bqhd,bkhd->bhqk/dot_general | solution.py:30
  1571.1 30.7 %multiply_add_fusion.5 = f32[8,6,512,128]{3,2,1,0:T(8,128)} fusion(f32[8,6,512,128]{3,2,1,0:T(8,128)} %get-tuple-element.143, f32[8,6,512]{2,1,0:T(8,128)S(1)} %get-tuple-element.130, bf16[8,512,2,6,128]{4,1,3,0,2:T(8,128)(2,1)} %collective-permute-done.1, f32[8,6,512,512]{2,3,1,0:T(8,128)} %get-tuple-element.128, f32[8,6,512]{2,1,0:T(8,128)S(1)} %max.4, ...), kind=kOutput, calls=%fused_computation.7.clone.1 | convolution fusion | flops 3290431488 | bytes 84082688 | tf_op jit(solution)/shard_map/while/body/eval_jaxpr/bhqk,bkhd->bhqd/dot_general | solution.py:37
  1604.3 135.5 %collective-permute-done = s32[8,512]{1,0:T(8,128)S(1)} collective-permute-done((s32[8,512]{1,0:T(8,128)S(1)}, s32[8,512]{1,0:T(8,128)S(1)}, u32[]{:S(2)}, u32[]{:S(2)}) %collective-permute-start) | collective-permute-done | bytes 16416 | tf_op jit(solution)/shard_map/while/body/eval_jaxpr/ppermute | solution.py:47
  1741.3 22.3 %fusion.40 = (f32[8,6,512]{2,1,0:T(8,128)S(1)}, f32[8,6,512,512]{2,3,1,0:T(8,128)}) fusion(pred[8,512,512]{1,2,0:T(8,128)(4,1)S(1)} %broadcast_compare_fusion.3, bf16[8,512,6,128]{3,1,2,0:T(8,128)(2,1)} %get-tuple-element.156, bf16[8,512,2,6,128]{4,1,3,0,2:T(8,128)(2,1)} %collective-permute-done.1), kind=kOutput, calls=%fused_computation.2.clone.1 | convolution fusion | flops 3258949632 | bytes 65110016 | tf_op jit(solution)/shard_map/while/body/eval_jaxpr/bqhd,bkhd->bhqk/dot_general | solution.py:30
  1797.0 30.7 %multiply_add_fusion.5 = f32[8,6,512,128]{3,2,1,0:T(8,128)} fusion(f32[8,6,512,128]{3,2,1,0:T(8,128)} %get-tuple-element.143, f32[8,6,512]{2,1,0:T(8,128)S(1)} %get-tuple-element.130, bf16[8,512,2,6,128]{4,1,3,0,2:T(8,128)(2,1)} %collective-permute-done.1, f32[8,6,512,512]{2,3,1,0:T(8,128)} %get-tuple-element.128, f32[8,6,512]{2,1,0:T(8,128)S(1)} %max.4, ...), kind=kOutput, calls=%fused_computation.7.clone.1 | convolution fusion | flops 3290431488 | bytes 84082688 | tf_op jit(solution)/shard_map/while/body/eval_jaxpr/bhqk,bkhd->bhqd/dot_general | solution.py:37
  1830.3 135.5 %collective-permute-done = s32[8,512]{1,0:T(8,128)S(1)} collective-permute-done((s32[8,512]{1,0:T(8,128)S(1)}, s32[8,512]{1,0:T(8,128)S(1)}, u32[]{:S(2)}, u32[]{:S(2)}) %collective-permute-start) | collective-permute-done | bytes 16416 | tf_op jit(solution)/shard_map/while/body/eval_jaxpr/ppermute | solution.py:47
  1967.2 22.3 %fusion.40 = (f32[8,6,512]{2,1,0:T(8,128)S(1)}, f32[8,6,512,512]{2,3,1,0:T(8,128)}) fusion(pred[8,512,512]{1,2,0:T(8,128)(4,1)S(1)} %broadcast_compare_fusion.3, bf16[8,512,6,128]{3,1,2,0:T(8,128)(2,1)} %get-tuple-element.156, bf16[8,512,2,6,128]{4,1,3,0,2:T(8,128)(2,1)} %collective-permute-done.1), kind=kOutput, calls=%fused_computation.2.clone.1 | convolution fusion | flops 3258949632 | bytes 65110016 | tf_op jit(solution)/shard_map/while/body/eval_jaxpr/bqhd,bkhd->bhqk/dot_general | solution.py:30
  1989.5 22.0 %fusion.41 = f32[8,6,512]{2,1,0:T(8,128)S(1)} fusion(f32[8,6,512,512]{2,3,1,0:T(8,128)} %get-tuple-element.128, f32[8,6,512]{2,1,0:T(8,128)S(1)} %max.4, pred[8,512,512]{1,2,0:T(8,128)(4,1)S(1)} %broadcast_compare_fusion.3), kind=kLoop, calls=%fused_computation.4.clone.1 | loop fusion | flops 62889984 | bytes 52625408 | tf_op jit(solution)/shard_map/while/body/eval_jaxpr/reduce_sum | solution.py:36
  2022.9 30.7 %multiply_add_fusion.5 = f32[8,6,512,128]{3,2,1,0:T(8,128)} fusion(f32[8,6,512,128]{3,2,1,0:T(8,128)} %get-tuple-element.143, f32[8,6,512]{2,1,0:T(8,128)S(1)} %get-tuple-element.130, bf16[8,512,2,6,128]{4,1,3,0,2:T(8,128)(2,1)} %collective-permute-done.1, f32[8,6,512,512]{2,3,1,0:T(8,128)} %get-tuple-element.128, f32[8,6,512]{2,1,0:T(8,128)S(1)} %max.4, ...), kind=kOutput, calls=%fused_computation.7.clone.1 | convolution fusion | flops 3290431488 | bytes 84082688 | tf_op jit(solution)/shard_map/while/body/eval_jaxpr/bhqk,bkhd->bhqd/dot_general | solution.py:37
  2066.5 72.8 %all_to_all.36 = bf16[8,6,512,128]{3,0,1,2:T(8,128)(2,1)S(1)} all-to-all(bf16[8,6,512,128]{3,0,1,2:T(8,128)(2,1)S(1)} %fusion.20), channel_id=1, replica_groups=mesh['dp'=1,'sp'=4,'cp'=8] {'sp'}, dimensions={2} | all-to-all | bytes 12582912 | tf_op jit(solution)/shard_map/all_to_all | solution.py:53
  2141.0 23.8 %bitcast_convert_fusion = bf16[8,128,3072]{2,1,0:T(8,128)(2,1)} fusion(bf16[8,24,128,128]{3,2,1,0:T(8,128)(2,1)S(1)} %bitcast.64, bf16[24,128,3072]{2,1,0:T(8,128)(2,1)} %param.9), kind=kOutput, calls=%fused_computation.27 | convolution fusion | flops 19330498560 | bytes 31457280 | tf_op jit(solution)/shard_map/bhnd,hdc->bnc/dot_general | solution.py:54
  (88 shorter events, 279.7 us)
Async XLA Ops:
  153.5 7.6 copy-start.2
  153.5 220.0 %all-to-all-start = ((bf16[8,128,3,24,128]{4,1,2,0,3:T(8,128)(2,1)}), bf16[8,128,3,24,128]{4,1,2,0,3:T(8,128)(2,1)}, u32[]{:S(2)}, u32[]{:S(2)}) async-start(bf16[8,128,3,24,128]{4,1,2,0,3:T(8,128)(2,1)} %copy.23), calls=%async_computation | async-start | bytes 37748736 | tf_op jit(solution)/shard_map/all_to_all | solution.py:21
  382.9 10.1 copy-start
  396.1 22.9 %copy-start.1 = (pred[8,512,512]{1,2,0:T(8,128)(4,1)S(1)}, pred[8,512,512]{1,2,0:T(8,128)(4,1)}, u32[]{:S(2)}) copy-start(pred[8,512,512]{1,2,0:T(8,128)(4,1)} %broadcast_compare_fusion.1) | copy-start | bytes 6291460
  469.1 142.5 %collective-permute-start.1 = (bf16[8,512,2,6,128]{4,1,3,0,2:T(8,128)(2,1)}, bf16[8,512,2,6,128]{4,1,3,0,2:T(8,128)(2,1)}, u32[]{:S(2)}, u32[]{:S(2)}) collective-permute-start(bf16[8,512,2,6,128]{4,1,3,0,2:T(8,128)(2,1)} %get-tuple-element.144), channel_id=1, source_target_pairs={{0,1},{1,2},{2,3},{3,4},{4,5},{5,6},{6,7},{7,0},{8,9},{9,10},{10,1... | collective-permute-start | bytes 37748744 | tf_op jit(solution)/shard_map/while/body/eval_jaxpr/ppermute | solution.py:46
  474.6 135.5 %collective-permute-start = (s32[8,512]{1,0:T(8,128)S(1)}, s32[8,512]{1,0:T(8,128)S(1)}, u32[]{:S(2)}, u32[]{:S(2)}) collective-permute-start(s32[8,512]{1,0:T(8,128)S(1)} %get-tuple-element.145), channel_id=1, source_target_pairs={{0,1},{1,2},{2,3},{3,4},{4,5},{5,6},{6,7},{7,0},{8,9},{9,10},{10,1... | collective-permute-start | bytes 49160 | tf_op jit(solution)/shard_map/while/body/eval_jaxpr/ppermute | solution.py:47
  698.1 139.5 %collective-permute-start.1 = (bf16[8,512,2,6,128]{4,1,3,0,2:T(8,128)(2,1)}, bf16[8,512,2,6,128]{4,1,3,0,2:T(8,128)(2,1)}, u32[]{:S(2)}, u32[]{:S(2)}) collective-permute-start(bf16[8,512,2,6,128]{4,1,3,0,2:T(8,128)(2,1)} %get-tuple-element.144), channel_id=1, source_target_pairs={{0,1},{1,2},{2,3},{3,4},{4,5},{5,6},{6,7},{7,0},{8,9},{9,10},{10,1... | collective-permute-start | bytes 37748744 | tf_op jit(solution)/shard_map/while/body/eval_jaxpr/ppermute | solution.py:46
  700.6 135.5 %collective-permute-start = (s32[8,512]{1,0:T(8,128)S(1)}, s32[8,512]{1,0:T(8,128)S(1)}, u32[]{:S(2)}, u32[]{:S(2)}) collective-permute-start(s32[8,512]{1,0:T(8,128)S(1)} %get-tuple-element.145), channel_id=1, source_target_pairs={{0,1},{1,2},{2,3},{3,4},{4,5},{5,6},{6,7},{7,0},{8,9},{9,10},{10,1... | collective-permute-start | bytes 49160 | tf_op jit(solution)/shard_map/while/body/eval_jaxpr/ppermute | solution.py:47
  924.0 139.4 %collective-permute-start.1 = (bf16[8,512,2,6,128]{4,1,3,0,2:T(8,128)(2,1)}, bf16[8,512,2,6,128]{4,1,3,0,2:T(8,128)(2,1)}, u32[]{:S(2)}, u32[]{:S(2)}) collective-permute-start(bf16[8,512,2,6,128]{4,1,3,0,2:T(8,128)(2,1)} %get-tuple-element.144), channel_id=1, source_target_pairs={{0,1},{1,2},{2,3},{3,4},{4,5},{5,6},{6,7},{7,0},{8,9},{9,10},{10,1... | collective-permute-start | bytes 37748744 | tf_op jit(solution)/shard_map/while/body/eval_jaxpr/ppermute | solution.py:46
  926.5 135.5 %collective-permute-start = (s32[8,512]{1,0:T(8,128)S(1)}, s32[8,512]{1,0:T(8,128)S(1)}, u32[]{:S(2)}, u32[]{:S(2)}) collective-permute-start(s32[8,512]{1,0:T(8,128)S(1)} %get-tuple-element.145), channel_id=1, source_target_pairs={{0,1},{1,2},{2,3},{3,4},{4,5},{5,6},{6,7},{7,0},{8,9},{9,10},{10,1... | collective-permute-start | bytes 49160 | tf_op jit(solution)/shard_map/while/body/eval_jaxpr/ppermute | solution.py:47
  1149.9 139.4 %collective-permute-start.1 = (bf16[8,512,2,6,128]{4,1,3,0,2:T(8,128)(2,1)}, bf16[8,512,2,6,128]{4,1,3,0,2:T(8,128)(2,1)}, u32[]{:S(2)}, u32[]{:S(2)}) collective-permute-start(bf16[8,512,2,6,128]{4,1,3,0,2:T(8,128)(2,1)} %get-tuple-element.144), channel_id=1, source_target_pairs={{0,1},{1,2},{2,3},{3,4},{4,5},{5,6},{6,7},{7,0},{8,9},{9,10},{10,1... | collective-permute-start | bytes 37748744 | tf_op jit(solution)/shard_map/while/body/eval_jaxpr/ppermute | solution.py:46
  1152.4 135.5 %collective-permute-start = (s32[8,512]{1,0:T(8,128)S(1)}, s32[8,512]{1,0:T(8,128)S(1)}, u32[]{:S(2)}, u32[]{:S(2)}) collective-permute-start(s32[8,512]{1,0:T(8,128)S(1)} %get-tuple-element.145), channel_id=1, source_target_pairs={{0,1},{1,2},{2,3},{3,4},{4,5},{5,6},{6,7},{7,0},{8,9},{9,10},{10,1... | collective-permute-start | bytes 49160 | tf_op jit(solution)/shard_map/while/body/eval_jaxpr/ppermute | solution.py:47
  1375.9 139.4 %collective-permute-start.1 = (bf16[8,512,2,6,128]{4,1,3,0,2:T(8,128)(2,1)}, bf16[8,512,2,6,128]{4,1,3,0,2:T(8,128)(2,1)}, u32[]{:S(2)}, u32[]{:S(2)}) collective-permute-start(bf16[8,512,2,6,128]{4,1,3,0,2:T(8,128)(2,1)} %get-tuple-element.144), channel_id=1, source_target_pairs={{0,1},{1,2},{2,3},{3,4},{4,5},{5,6},{6,7},{7,0},{8,9},{9,10},{10,1... | collective-permute-start | bytes 37748744 | tf_op jit(solution)/shard_map/while/body/eval_jaxpr/ppermute | solution.py:46
  1378.4 135.5 %collective-permute-start = (s32[8,512]{1,0:T(8,128)S(1)}, s32[8,512]{1,0:T(8,128)S(1)}, u32[]{:S(2)}, u32[]{:S(2)}) collective-permute-start(s32[8,512]{1,0:T(8,128)S(1)} %get-tuple-element.145), channel_id=1, source_target_pairs={{0,1},{1,2},{2,3},{3,4},{4,5},{5,6},{6,7},{7,0},{8,9},{9,10},{10,1... | collective-permute-start | bytes 49160 | tf_op jit(solution)/shard_map/while/body/eval_jaxpr/ppermute | solution.py:47
  1601.8 139.4 %collective-permute-start.1 = (bf16[8,512,2,6,128]{4,1,3,0,2:T(8,128)(2,1)}, bf16[8,512,2,6,128]{4,1,3,0,2:T(8,128)(2,1)}, u32[]{:S(2)}, u32[]{:S(2)}) collective-permute-start(bf16[8,512,2,6,128]{4,1,3,0,2:T(8,128)(2,1)} %get-tuple-element.144), channel_id=1, source_target_pairs={{0,1},{1,2},{2,3},{3,4},{4,5},{5,6},{6,7},{7,0},{8,9},{9,10},{10,1... | collective-permute-start | bytes 37748744 | tf_op jit(solution)/shard_map/while/body/eval_jaxpr/ppermute | solution.py:46
  1604.3 135.5 %collective-permute-start = (s32[8,512]{1,0:T(8,128)S(1)}, s32[8,512]{1,0:T(8,128)S(1)}, u32[]{:S(2)}, u32[]{:S(2)}) collective-permute-start(s32[8,512]{1,0:T(8,128)S(1)} %get-tuple-element.145), channel_id=1, source_target_pairs={{0,1},{1,2},{2,3},{3,4},{4,5},{5,6},{6,7},{7,0},{8,9},{9,10},{10,1... | collective-permute-start | bytes 49160 | tf_op jit(solution)/shard_map/while/body/eval_jaxpr/ppermute | solution.py:47
  1827.8 139.4 %collective-permute-start.1 = (bf16[8,512,2,6,128]{4,1,3,0,2:T(8,128)(2,1)}, bf16[8,512,2,6,128]{4,1,3,0,2:T(8,128)(2,1)}, u32[]{:S(2)}, u32[]{:S(2)}) collective-permute-start(bf16[8,512,2,6,128]{4,1,3,0,2:T(8,128)(2,1)} %get-tuple-element.144), channel_id=1, source_target_pairs={{0,1},{1,2},{2,3},{3,4},{4,5},{5,6},{6,7},{7,0},{8,9},{9,10},{10,1... | collective-permute-start | bytes 37748744 | tf_op jit(solution)/shard_map/while/body/eval_jaxpr/ppermute | solution.py:46
  1830.3 135.5 %collective-permute-start = (s32[8,512]{1,0:T(8,128)S(1)}, s32[8,512]{1,0:T(8,128)S(1)}, u32[]{:S(2)}, u32[]{:S(2)}) collective-permute-start(s32[8,512]{1,0:T(8,128)S(1)} %get-tuple-element.145), channel_id=1, source_target_pairs={{0,1},{1,2},{2,3},{3,4},{4,5},{5,6},{6,7},{7,0},{8,9},{9,10},{10,1... | collective-permute-start | bytes 49160 | tf_op jit(solution)/shard_map/while/body/eval_jaxpr/ppermute | solution.py:47
where the time goes:
time: 2170 us; the launch traced here: 2160 us
  waiting for transfers between devices  948 us (44%)
  matrix products  510 us (24%)
  blocking collectives  283 us (13%)
  other arithmetic  202 us (9%)
  local copies, waits for them, and re-layouts  193 us (9%)
  starting transfers between devices  28.3 us (1%)
    ppermute x7, waiting for transfers between devices, pass_step(): seg_cur = lax.ppermute(seg_cur, 'cp', shift_pairs)  948 us
    dot_general x8, matrix products, absorb(): jnp.einsum('bhqk,bkhd->bhqd', weights.astype(jnp.bfloat16), kv_blk[:, :,...  243 us
    all_gather x1, blocking collectives, local_layer(): seg_query = lax.all_gather(seg_ids, 'sp', axis=1, tiled=True)  210 us
    dot_general x8, matrix products, absorb(): jnp.einsum('bqhd,bkhd->bhqk', queries, kv_blk[:, :, 0], preferred_element...  179 us
    reduce_sum x8, other arithmetic, absorb(): run_sum = run_sum * rescale + jnp.sum(weights, axis=-1)  176 us
    while x21, local copies, waits for them, and re-layouts  79 us
    reshape x1, local copies, waits for them, and re-layouts, local_layer(): w_qkv.reshape(model_dim, 3 * num_heads * head_dim)  77 us
    all_to_all x1, blocking collectives, local_layer(): attn_out = lax.all_to_all(attn_out, 'sp', 2, 1, tiled=True)  72.8 us
  transfers between devices with their start and end apart: 15, of which 7 were waited for; matrix products, arithmetic and copies ran while one was open for 1% of the time, Pallas kernels for 0%

commit v1 on v0

v1 whole, which is shorter than its diff:
```python
import functools
import math

import jax
import jax.numpy as jnp
from jax import lax
from jax.experimental import pallas as pl
from jax.experimental.pallas import tpu as pltpu
from jax.sharding import PartitionSpec as P

MESH = pl.DeviceIdType.MESH
NEG = -3.3e38
CORES = 2


def place(rank, lane):
    return rank // CORES, rank % CORES, lane // 2, lane % 2


def gather_project_kernel(cols, hid, w_hbm, out, blocks, w_vmem, stage, recv_sem, direct_sem, relay_sem, twin_sem,
                          w_sem, own_sem, out_sem):
    rank, lane = lax.axis_index('cp'), lax.axis_index('sp')
    columns = cols
    x, core, pair, end = place(rank, lane)
    far = 3 - lane
    mate = 2 * pair + 1 - end

    def dev(xx, cc, yy):
        return {'cp': xx * CORES + cc, 'sp': yy}

    def slot_of(xx, hh, cc, ee):
        return ((xx * 2 + hh) * CORES + cc) * 2 + ee

    me = slot_of(x, pair, core, end)
    steps = [(dx, other) for dx in (0, 1, columns - 1, 2) for other in (0, 1)]
    twin = dev(x, 1 - core, lane)
    partner = dev(x, core, mate)

    barrier = pltpu.get_barrier_semaphore()
    targets = [dev((x + columns - dx) % columns, core, far if other else lane) for dx, other in steps[1:]]
    for target in targets + [partner, twin]:
        pl.semaphore_signal(barrier, inc=1, device_id=target, device_id_type=MESH)

    own_seq = x * 2 + pair
    own = pltpu.make_async_copy(hid.at[own_seq], blocks.at[me], own_sem)
    own.start()
    w_copy = pltpu.make_async_copy(w_hbm, w_vmem, w_sem)
    w_copy.start()
    pl.semaphore_wait(barrier, len(targets) + 2)

    directs = []
    for i, (dx, other) in enumerate(steps[1:]):
        xt = (x + columns - dx) % columns
        seq = xt * 2 + (1 - pair if other else pair)
        copy = pltpu.make_async_remote_copy(
            src_ref=hid.at[seq], dst_ref=blocks.at[me], send_sem=direct_sem.at[i], recv_sem=recv_sem.at[me],
            device_id=targets[i], device_id_type=MESH)
        copy.start()
        directs.append(copy)

    def remote(slot, sem, device):
        return pltpu.make_async_remote_copy(
            src_ref=blocks.at[slot], dst_ref=blocks.at[slot], send_sem=sem, recv_sem=recv_sem.at[slot],
            device_id=device, device_id_type=MESH)

    own.wait()
    rows = stage.shape[1] // 4
    depth, width = w_vmem.shape
    tile = 256

    def out_copies(j, xs, hs):
        buf = j % 2
        return [pltpu.make_async_copy(
            stage.at[buf, pl.ds(k * rows, rows)],
            out.at[pl.ds(pl.multiple_of(((xs * CORES + k // 2) * 4 + hs * 2 + k % 2) * rows, rows), rows)],
            out_sem.at[buf, k]) for k in range(4)]

    def group(j):
        s = j // 2
        dx = s + jnp.where(s == 2, 1, 0) - jnp.where(s == 3, 1, 0)
        xs = (x + dx) % columns
        hs = (pair + j % 2) % 2
        return xs, hs

    def step(j, carry):
        xs, hs = group(j)
        de = jnp.where(j % 2 == 0, end, 1 - end)
        direct = slot_of(xs, hs, core, de)
        via = slot_of(xs, hs, core, 1 - de)

        @pl.when(j > 0)
        def _():
            remote(direct, relay_sem.at[j], partner).wait_recv()

        remote(direct, relay_sem.at[j], partner).start()
        remote(direct, twin_sem.at[j, 0], twin).start()
        remote(via, twin_sem.at[j, 1], twin).wait_recv()
        remote(via, twin_sem.at[j, 1], twin).start()
        remote(slot_of(xs, hs, 1 - core, de), twin_sem.at[j, 0], twin).wait_recv()
        remote(slot_of(xs, hs, 1 - core, 1 - de), twin_sem.at[j, 1], twin).wait_recv()

        @pl.when(j == 0)
        def _():
            w_copy.wait()

        @pl.when(j >= 2)
        def _():
            for copy in out_copies(j, *group(j - 2)):
                copy.wait()

        base = slot_of(xs, hs, 0, 0)
        lhs = blocks.at[pl.ds(base, 4)]
        buf = j % 2

        def column(n, carry):
            c = pl.ds(pl.multiple_of(n * tile, tile), tile)
            acc = jnp.dot(lhs[...].reshape(4 * rows, depth), w_vmem[:, c], preferred_element_type=jnp.float32)
            stage[buf, :, c] = acc.astype(jnp.bfloat16)
            return carry

        lax.fori_loop(0, width // tile, column, 0)
        for copy in out_copies(j, xs, hs):
            copy.start()
        return carry

    n_groups = len(steps)
    lax.fori_loop(0, n_groups, step, 0)

    for copy in directs:
        copy.wait_send()

    def drain(j, carry):
        xs, hs = group(j)
        remote(me, relay_sem.at[j], partner).wait_send()
        remote(me, twin_sem.at[j, 0], twin).wait_send()
        remote(me, twin_sem.at[j, 1], twin).wait_send()

        @pl.when(j >= n_groups - 2)
        def _():
            for copy in out_copies(j, xs, hs):
                copy.wait()

        return carry

    lax.fori_loop(0, n_groups, drain, 0)


def gather_project(hidden, w_local, columns, n_blocks):
    batch, tokens, depth = hidden.shape
    width = w_local.shape[1]
    n_groups = n_blocks // 4
    return pl.pallas_call(
        functools.partial(gather_project_kernel, columns),
        out_shape=jax.ShapeDtypeStruct((n_blocks * tokens, width), jnp.bfloat16),
        in_specs=[pl.BlockSpec(memory_space=pl.ANY)] * 2,
        out_specs=pl.BlockSpec(memory_space=pl.ANY),
        scratch_shapes=[
            pltpu.VMEM((n_blocks, tokens, depth), jnp.bfloat16),
            pltpu.VMEM((depth, width), jnp.bfloat16),
            pltpu.VMEM((2, 4 * tokens, width), jnp.bfloat16),
            pltpu.SemaphoreType.DMA((n_blocks,)),
            pltpu.SemaphoreType.DMA((n_groups - 1,)),
            pltpu.SemaphoreType.DMA((n_groups,)),
            pltpu.SemaphoreType.DMA((n_groups, 2)),
            pltpu.SemaphoreType.DMA,
            pltpu.SemaphoreType.DMA,
            pltpu.SemaphoreType.DMA((2, 4)),
        ],
        compiler_params=pltpu.CompilerParams(collective_id=0, has_side_effects=True, vmem_limit_bytes=60 * 2**20),
        name='gather_project',
    )(hidden, w_local)


def attention_kernel(tk, scale2, bounds, q_ref, k_ref, v_ref, segq_ref, segk_ref, o_ref, vt, s_buf):
    i = pl.program_id(1)
    tq, head_dim = q_ref.shape

    @pl.when(i == 0)
    def _():
        vt[...] = v_ref[...].T

    lo, full_lo, full_hi, hi = (bounds[n, i] for n in range(4))
    q = q_ref[...]

    def scores(chunk, slot):
        k = k_ref[pl.ds(pl.multiple_of(chunk * tk, tk), tk), :]
        s_buf[slot] = lax.dot_general(k, q, (((1,), (1,)), ((), ())), preferred_element_type=jnp.float32)

    def absorb(chunk, slot, state, masked):
        m, l, acc = state
        at = pl.ds(pl.multiple_of(chunk * tk, tk), tk)
        s = s_buf[slot]
        if masked:
            allowed = segk_ref[at, :1] == segq_ref[:1, :]
            s = jnp.where(allowed, s, NEG)
        m_new = jnp.maximum(m, jnp.max(s, axis=0, keepdims=True))
        p = jnp.exp2((s - m_new) * scale2)
        if masked:
            p = jnp.where(allowed, p, 0.0)
        alpha = jnp.exp2((m - m_new) * scale2)
        l = l * alpha + jnp.sum(p, axis=0, keepdims=True)
        acc = acc * alpha + lax.dot_general(vt[:, at], p.astype(jnp.bfloat16), (((1,), (0,)), ((), ())),
                                            preferred_element_type=jnp.float32)
        return m_new, l, acc

    head = full_lo - lo
    n_masked = head + hi - full_hi

    def masked_step(n, state):
        chunk = jnp.where(n < head, lo + n, full_hi + n - head)
        scores(chunk, 0)
        return absorb(chunk, 0, state, True)

    def full_step(n, state):
        slot = (n - full_lo) % 2

        scores(jnp.minimum(n + 1, full_hi - 1), 1 - slot)
        return absorb(n, slot, state, False)

    state = (jnp.full((1, tq), NEG, jnp.float32), jnp.zeros((1, tq), jnp.float32),
             jnp.zeros((head_dim, tq), jnp.float32))
    state = lax.fori_loop(0, n_masked, masked_step, state)

    @pl.when(full_hi > full_lo)
    def _():
        scores(full_lo, 0)

    m, l, acc = lax.fori_loop(full_lo, full_hi, full_step, state)
    o_ref[...] = (acc / l).T.astype(o_ref.dtype)


def attention(qkv, seg, heads, head_dim, tq, tk):
    length = qkv.shape[0]
    n_q = length // tq
    first, last = seg[::tq], seg[tq - 1::tq]
    start = jnp.sum(seg[None, :] < first[:, None], axis=1)
    stop = jnp.sum(seg[None, :] <= last[:, None], axis=1)
    lo, hi = start // tk, (stop + tk - 1) // tk
    full_lo, full_hi = (start + tk - 1) // tk, stop // tk
    plain = (first == last) & (full_hi > full_lo)
    full_lo = jnp.where(plain, full_lo, hi)
    full_hi = jnp.where(plain, full_hi, hi)
    bounds = jnp.stack([lo, full_lo, full_hi, hi]).astype(jnp.int32)
    segq = jnp.broadcast_to(seg[None, :], (8, length))
    segk = jnp.broadcast_to(seg[:, None], (length, 128))
    scale2 = head_dim ** -0.5 * math.log2(math.e)
    return pl.pallas_call(
        functools.partial(attention_kernel, tk, scale2),
        out_shape=jax.ShapeDtypeStruct((length, heads * head_dim), jnp.bfloat16),
        grid_spec=pltpu.PrefetchScalarGridSpec(
            num_scalar_prefetch=1, grid=(heads, n_q),
            in_specs=[
                pl.BlockSpec((tq, head_dim), lambda h, i, b: (i, h)),
                pl.BlockSpec((length, head_dim), lambda h, i, b: (0, heads + h)),
                pl.BlockSpec((length, head_dim), lambda h, i, b: (0, 2 * heads + h)),
                pl.BlockSpec((8, tq), lambda h, i, b: (0, i)),
                pl.BlockSpec((length, 128), lambda h, i, b: (0, 0)),
            ],
            out_specs=pl.BlockSpec((tq, head_dim), lambda h, i, b: (i, h)),
            scratch_shapes=[
                pltpu.VMEM((head_dim, length), jnp.bfloat16),
                pltpu.VMEM((2, tk, tq), jnp.float32),
            ]),
        compiler_params=pltpu.CompilerParams(vmem_limit_bytes=48 * 2**20),
        name='attention',
    )(bounds, qkv, qkv, qkv, segq, segk)


def solution(mesh):
    n_cp, n_sp = mesh.shape['cp'], mesh.shape['sp']
    n_blocks = n_cp * n_sp
    columns = n_cp // CORES
    token_spec = P('dp', ('cp', 'sp'), None)
    seg_spec = P('dp', ('cp', 'sp'))

    def local_layer(hidden, seg_ids, w_qkv, w_out):
        batch, tokens, depth = hidden.shape
        n_heads, head_dim = w_out.shape[:2]
        groups = n_blocks // batch
        assert n_sp == 4 and columns == 4 and groups == 4 and batch == 2 * columns
        heads = n_heads // groups
        x, core, pair, end = place(lax.axis_index('cp'), lax.axis_index('sp'))
        group = core * 2 + end
        seq = x * 2 + pair
        w_local = lax.dynamic_slice(w_qkv, (0, 0, group * heads, 0), (depth, 3, heads, head_dim))
        w_local = w_local.reshape(depth, 3 * heads * head_dim)
        qkv = gather_project(hidden, w_local, columns, n_blocks)

        seg = lax.all_gather(seg_ids, ('cp', 'sp'), axis=1, tiled=True)
        seg = lax.dynamic_slice(seg, (seq, 0), (1, tokens * n_blocks))[0]
        o = attention(qkv, seg, heads, head_dim, 512, 512)

        o = o.reshape(n_blocks, tokens, heads * head_dim)
        o = lax.all_to_all(o, ('cp', 'sp'), 0, 0, tiled=True)
        o = o.reshape(columns, CORES, 2, 2, tokens, heads * head_dim)
        o = o.transpose(0, 2, 4, 1, 3, 5).reshape(batch, tokens, n_heads * head_dim)
        y = jnp.dot(o, w_out.reshape(n_heads * head_dim, depth), preferred_element_type=jnp.float32)
        return y.astype(jnp.bfloat16)

    return jax.shard_map(local_layer, mesh=mesh, in_specs=(token_spec, seg_spec, P(), P()), out_specs=token_spec,
                         check_vma=False)
```

time: 2170 us -> 738 us (0.34)
  waiting for transfers between devices: 948 us -> 0 us
  matrix products: 510 us -> 25.5 us
  Pallas kernels: 0 us -> 473 us
  other arithmetic: 202 us -> 0.3 us
  blocking collectives: 283 us -> 154 us
  local copies, waits for them, and re-layouts: 193 us -> 84 us
  starting transfers between devices: 28.3 us -> 0 us
    ppermute x14 -> x0, waiting for transfers between devices: 948 us -> none  [the longest x7 948 us: pass_step(): seg_cur = lax.ppermute(seg_cur, 'cp', shift_pairs)]
    dot_general x18 -> x1, matrix products: 510 us -> 25.5 us  [local_layer(): jnp.dot(o, w_out.reshape(n_heads * head_dim, depth), preferred_element_ty...]
    pallas_call x0 -> x2, Pallas kernels: none -> 473 us  [the longest x1 254 us: gather_project(): pl.pallas_call(functools.partial(gather_project_kernel, columns), out_sha...]
    all_gather x1, blocking collectives: 210 us -> 30.3 us  [local_layer(): seg = lax.all_gather(seg_ids, ('cp', 'sp'), axis=1, tiled=True)]
    reduce_sum x8 -> x1, other arithmetic: 176 us -> 0.25 us  [attention(): start = jnp.sum(seg[None, :] < first[:, None], axis=1)]
    while x22 -> x0, local copies, waits for them, and re-layouts: 79.8 us -> none
    all_to_all x1, blocking collectives: 72.8 us -> 123 us  [local_layer(): o = lax.all_to_all(o, ('cp', 'sp'), 0, 0, tiled=True)]
    reshape x2 -> x3, local copies, waits for them, and re-layouts: 84.3 us -> 38.1 us  [the longest x1 17.8 us: local_layer(): w_local = w_local.reshape(depth, 3 * heads * head_dim)]
  transfers between devices with their start and end apart: 15 -> 0, of which waited for: 7 -> 0; matrix products, arithmetic and copies ran while one was open for 1% -> 0% of each run, Pallas kernels for 0% -> 0%
where the time goes in v1:
time: 738 us; the launch traced here: 736 us
  Pallas kernels  473 us (64%)
  blocking collectives  154 us (21%)
  local copies, waits for them, and re-layouts  84 us (11%)
  matrix products  25.5 us (3%)
    pallas_call x1, Pallas kernels, gather_project(): pl.pallas_call(functools.partial(gather_project_kernel, columns), out_sha...  254 us
    pallas_call x1, Pallas kernels, attention(): pl.pallas_call(functools.partial(attention_kernel, tk, scale2), out_shape...  219 us
    all_to_all x1, blocking collectives, local_layer(): o = lax.all_to_all(o, ('cp', 'sp'), 0, 0, tiled=True)  123 us
    all_gather x1, blocking collectives, local_layer(): seg = lax.all_gather(seg_ids, ('cp', 'sp'), axis=1, tiled=True)  30.3 us
    dot_general x1, matrix products, local_layer(): jnp.dot(o, w_out.reshape(n_heads * head_dim, depth), preferred_element_ty...  25.5 us
    unnamed x1, local copies, waits for them, and re-layouts  22.6 us
    dynamic_slice x1, local copies, waits for them, and re-layouts, local_layer(): lax.dynamic_slice(w_qkv, (0, 0, group * heads, 0), (depth, 3, heads, head...  22.5 us
    reshape x1, local copies, waits for them, and re-layouts, local_layer(): w_local = w_local.reshape(depth, 3 * heads * head_dim)  17.8 us

profile of v1, /device:TPU:99, one launch (start us, length us, event | category | flops | bytes accessed | tf_op | source)
XLA Modules:
  0.0 736.5 jit_solution(3051590954173015794)
XLA Ops:
  0.0 30.3 %all_gather.3 = s32[8,4096]{1,0:T(8,128)S(1)} all-gather(s32[8,128]{1,0:T(8,128)} %param.5), channel_id=1, replica_groups=mesh['dp'=1,'sp'=4,'cp'=8] {'cp','sp'}, dimensions={1}, use_global_device_ids=true | all-gather | bytes 135168 | tf_op jit(solution)/shard_map/all_gather | solution.py:289
  30.3 0.1 slice.6
  30.4 0.1 slice.7
  30.5 0.3 convert_reduce_fusion.1
  30.8 22.5 %constant_dynamic-slice_fusion = bf16[3072,3,6,128]{3,2,1,0:T(8,128)(2,1)} fusion(bf16[3072,3,24,128]{3,2,1,0:T(8,128)(2,1)} %param.6, s32[]{:T(128)S(6)} %select_n.72), kind=kLoop, calls=%fused_computation.30 | loop fusion | bytes 28311556 | tf_op jit(solution)/shard_map/dynamic_slice | solution.py:285
  53.4 22.6 %copy.9 = bf16[3072,3,6,128]{0,3,2,1:T(8,128)(2,1)} copy(bf16[3072,3,6,128]{3,2,1,0:T(8,128)(2,1)} %constant_dynamic-slice_fusion) | data formatting | bytes 28311552
  76.0 17.8 %copy.7.w_hbm = bf16[3072,2304]{1,0:T(8,128)(2,1)} copy(bf16[3072,2304]{0,1:T(8,128)(2,1)} %bitcast.32) | data formatting | bytes 28311552 | tf_op jit(solution)/shard_map/reshape | solution.py:286
  93.7 253.7 %gather_project.1.q_ref.k_ref.v_ref = bf16[4096,2304]{1,0:T(8,128)(2,1)} custom-call(bf16[8,128,3072]{2,1,0:T(8,128)(2,1)} %hid.1, bf16[3072,2304]{1,0:T(8,128)(2,1)} %copy.7.w_hbm), custom_call_target="tpu_custom_call" | custom-call | tf_op jit(solution)/shard_map/gather_project/pallas_call | solution.py:152
  347.5 0.6 broadcast_in_dim.2.segk_ref
  348.1 219.3 %attention.1 = bf16[4096,768]{1,0:T(8,128)(2,1)} custom-call(s32[4,8]{1,0:T(4,128)S(1)} %pad_add_fusion.bounds, bf16[4096,2304]{1,0:T(8,128)(2,1)} %gather_project.1.q_ref.k_ref.v_ref, bf16[4096,2304]{1,0:T(8,128)(2,1)} %gather_project.1.q_ref.k_ref.v_ref, bf16[4096,2304]{1,0:T(8,128)(2,1)} %gather_project.1.q_ref.k_ref.v_ref, s32[8,4096]{1,0:T(8,128)S(1)} %lt.33.segq_ref, ...), custom_call_target="tpu_custom_call" | custom-call | tf_op jit(solution)/shard_map/attention/pallas_call | solution.py:247
  567.3 123.2 %all_to_all.5 = bf16[32,128,768]{2,1,0:T(8,128)(2,1)S(1)} all-to-all(bf16[32,128,768]{2,1,0:T(8,128)(2,1)} %bitcast.33), channel_id=1, replica_groups=mesh['dp'=1,'sp'=4,'cp'=8] {'cp','sp'}, dimensions={0} | all-to-all | bytes 12582912 | tf_op jit(solution)/shard_map/all_to_all | solution.py:294
  690.6 5.9 copy.11
  696.5 14.4 %reshape.124 = bf16[8,128,3072]{2,1,0:T(8,128)(2,1)} reshape(bf16[4,2,128,2,2,768]{5,4,3,2,1,0:T(2,128)(2,1)} %bitcast.35) | data formatting | bytes 12582912 | tf_op jit(solution)/shard_map/reshape | solution.py:296
  710.9 25.5 %convolution_convert_fusion = bf16[8,128,3072]{2,1,0:T(8,128)(2,1)} fusion(bf16[8,128,3072]{2,1,0:T(8,128)(2,1)} %reshape.124, bf16[3072,3072,1]{1,0,2:T(8,128)(2,1)} %bitcast.41), kind=kOutput, calls=%fused_computation.1 | convolution fusion | flops 19330498560 | bytes 31457280 | tf_op jit(solution)/shard_map/dot_general | solution.py:297
  (6 shorter events, 0.1 us)

commit v2 on v1

v2 whole, which is shorter than its diff:
```python
import functools
import math

import jax
import jax.numpy as jnp
from jax import lax
from jax.experimental import pallas as pl
from jax.experimental.pallas import tpu as pltpu
from jax.sharding import PartitionSpec as P

MESH = pl.DeviceIdType.MESH
CORES = 2


def place(rank, lane):
    return rank // CORES, rank % CORES, lane // 2, lane % 2


def gather_project_kernel(columns, heads, hid, seg, w_hbm, out, seg_out, blocks, w_vmem, stage, w_in, w_wide, recv_sem,
                          direct_sem, relay_sem, twin_sem, w_sem, own_sem, out_sem, seg_send, seg_recv):
    rank, lane = lax.axis_index('cp'), lax.axis_index('sp')
    x, core, pair, end = place(rank, lane)
    far = 3 - lane
    mate = 2 * pair + 1 - end
    n_blocks = blocks.shape[0]
    lanes = n_blocks // (columns * CORES)

    def dev(xx, cc, yy):
        return {'cp': xx * CORES + cc, 'sp': yy}

    def slot_of(xx, hh, cc, ee):
        return ((xx * 2 + hh) * CORES + cc) * 2 + ee

    me = slot_of(x, pair, core, end)
    steps = [(dx, other) for dx in (0, 1, columns - 1, 2) for other in (0, 1)]
    n_groups = len(steps)
    twin = dev(x, 1 - core, lane)
    partner = dev(x, core, mate)

    def peer(k):
        p = (rank * lanes + lane + k) % n_blocks
        return {'cp': p // lanes, 'sp': p % lanes}

    barrier = pltpu.get_barrier_semaphore()

    def greet(k, carry):
        pl.semaphore_signal(barrier, inc=1, device_id=peer(k), device_id_type=MESH)
        return carry

    lax.fori_loop(1, n_blocks, greet, 0)

    own = pltpu.make_async_copy(hid.at[x * 2 + pair], blocks.at[me], own_sem.at[0])
    own.start()
    here = rank * lanes + lane
    own_seg = pltpu.make_async_copy(seg, seg_out.at[here], own_sem.at[1])
    own_seg.start()

    first = (core * 2 + end) * heads
    tile0 = jnp.minimum(first // 8, w_hbm.shape[2] // 8 - 2) * 8
    shift = first - tile0
    depth, width = w_vmem.shape
    chunk = w_in.shape[1]

    def w_copy(n):
        return pltpu.make_async_copy(
            w_hbm.at[pl.ds(pl.multiple_of(n * chunk, chunk), chunk), :, pl.ds(pl.multiple_of(tile0, 8), 16), :],
            w_in.at[n % 2], w_sem.at[n % 2])

    w_copy(0).start()
    pl.semaphore_wait(barrier, n_blocks - 1)

    directs = []
    for i, (dx, other) in enumerate(steps[1:]):
        xt = (x + columns - dx) % columns
        copy = pltpu.make_async_remote_copy(
            src_ref=hid.at[xt * 2 + (1 - pair if other else pair)], dst_ref=blocks.at[me], send_sem=direct_sem.at[i],
            recv_sem=recv_sem.at[me], device_id=dev(xt, core, far if other else lane), device_id_type=MESH)
        copy.start()
        directs.append(copy)

    def remote(slot, sem, device):
        return pltpu.make_async_remote_copy(
            src_ref=blocks.at[slot], dst_ref=blocks.at[slot], send_sem=sem, recv_sem=recv_sem.at[slot],
            device_id=device, device_id_type=MESH)

    def group(j):
        s = j // 2
        dx = s + jnp.where(s == 2, 1, 0) - jnp.where(s == 3, 1, 0)
        return (x + dx) % columns, (pair + j % 2) % 2

    def sides(j):
        de = jnp.where(j % 2 == 0, end, 1 - end)
        return de, 1 - de

    def serve(j):
        xs, hs = group(j)
        slot = slot_of(xs, hs, core, sides(j)[0])

        @pl.when(j > 0)
        def _():
            remote(slot, relay_sem.at[j], partner).wait_recv()

        remote(slot, relay_sem.at[j], partner).start()
        remote(slot, twin_sem.at[j, 0], twin).start()

    own.wait()
    serve(0)

    def send_seg(k, carry):
        pltpu.make_async_remote_copy(src_ref=seg, dst_ref=seg_out.at[here], send_sem=seg_send, recv_sem=seg_recv,
                                     device_id=peer(k), device_id_type=MESH).start()
        return carry

    lax.fori_loop(1, n_blocks, send_seg, 0)

    n_chunks = depth // chunk
    lane_width = w_wide.shape[1]

    def relay_weights(n, carry):
        @pl.when(n + 1 < n_chunks)
        def _():
            w_copy(n + 1).start()

        w_copy(n).wait()
        half = chunk * 8
        for kind in range(3):
            both = w_in[n % 2, :, kind].astype(jnp.float32)
            for part in range(2):
                w_wide[pl.ds((2 * kind + part) * half, half), :] = both[:, part * 8:part * 8 + 8].reshape(half, lane_width)
        for kind in range(3):
            for h in range(heads):
                row = (2 * kind + (shift + h) // 8) * half + (shift + h) % 8
                at = (kind * heads + h) * lane_width
                w_vmem[pl.ds(pl.multiple_of(n * chunk, chunk), chunk), pl.ds(at, lane_width)] = (
                    w_wide[pl.ds(row, chunk, stride=8), :].astype(jnp.bfloat16))
        return carry

    lax.fori_loop(0, n_chunks // 2, relay_weights, 0)
    serve(1)
    lax.fori_loop(n_chunks // 2, n_chunks, relay_weights, 0)

    rows = stage.shape[1] // 4
    tile = 256

    def out_copies(j):
        xs, hs = group(j)
        buf = j % 2
        return [pltpu.make_async_copy(
            stage.at[buf, pl.ds(k * rows, rows)],
            out.at[pl.ds(pl.multiple_of(((xs * CORES + k // 2) * lanes + hs * 2 + k % 2) * rows, rows), rows)],
            out_sem.at[buf, k]) for k in range(4)]

    def step(j, carry):
        xs, hs = group(j)
        de, ve = sides(j)

        @pl.when(j + 2 < n_groups)
        def _():
            serve(j + 2)

        via = slot_of(xs, hs, core, ve)
        remote(via, twin_sem.at[j, 1], twin).wait_recv()
        remote(via, twin_sem.at[j, 1], twin).start()
        remote(slot_of(xs, hs, 1 - core, de), twin_sem.at[j, 0], twin).wait_recv()
        remote(slot_of(xs, hs, 1 - core, ve), twin_sem.at[j, 1], twin).wait_recv()

        @pl.when(j >= 2)
        def _():
            for copy in out_copies(j - 2):
                copy.wait()

        lhs = blocks.at[pl.ds(slot_of(xs, hs, 0, 0), 4)]
        buf = j % 2

        def column(n, carry):
            c = pl.ds(pl.multiple_of(n * tile, tile), tile)
            acc = jnp.dot(lhs[...].reshape(4 * rows, depth), w_vmem[:, c], preferred_element_type=jnp.float32)
            stage[buf, :, c] = acc.astype(jnp.bfloat16)
            return carry

        lax.fori_loop(0, width // tile, column, 0)
        for copy in out_copies(j):
            copy.start()
        return carry

    lax.fori_loop(0, n_groups, step, 0)

    for copy in directs:
        copy.wait_send()

    def drain(j, carry):
        remote(me, relay_sem.at[j], partner).wait_send()
        remote(me, twin_sem.at[j, 0], twin).wait_send()
        remote(me, twin_sem.at[j, 1], twin).wait_send()

        @pl.when(j >= n_groups - 2)
        def _():
            for copy in out_copies(j):
                copy.wait()

        return carry

    lax.fori_loop(0, n_groups, drain, 0)
    others = seg_out.at[pl.ds(0, n_blocks - 1)]
    all_segs = pltpu.make_async_remote_copy(src_ref=others, dst_ref=others, send_sem=seg_send, recv_sem=seg_recv,
                                            device_id=twin, device_id_type=MESH)
    all_segs.wait_send()
    all_segs.wait_recv()
    own_seg.wait()


def gather_project(hidden, seg_ids, w_qkv, heads, columns, n_blocks):
    batch, tokens, depth = hidden.shape
    head_dim = w_qkv.shape[3]
    width = 3 * heads * head_dim
    n_groups = n_blocks // 4
    chunk = 64 if depth % 128 == 0 else depth
    return pl.pallas_call(
        functools.partial(gather_project_kernel, columns, heads),
        out_shape=(jax.ShapeDtypeStruct((n_blocks * tokens, width), jnp.bfloat16),
                   jax.ShapeDtypeStruct((n_blocks,) + seg_ids.shape, seg_ids.dtype)),
        in_specs=[pl.BlockSpec(memory_space=pl.ANY)] * 3,
        out_specs=[pl.BlockSpec(memory_space=pl.ANY)] * 2,
        scratch_shapes=[
            pltpu.VMEM((n_blocks, tokens, depth), jnp.bfloat16),
            pltpu.VMEM((depth, width), jnp.bfloat16),
            pltpu.VMEM((2, 4 * tokens, width), jnp.bfloat16),
            pltpu.VMEM((2, chunk, 3, 16, head_dim), jnp.bfloat16),
            pltpu.VMEM((3 * 16 * chunk, head_dim), jnp.float32),
            pltpu.SemaphoreType.DMA((n_blocks,)),
            pltpu.SemaphoreType.DMA((n_groups - 1,)),
            pltpu.SemaphoreType.DMA((n_groups,)),
            pltpu.SemaphoreType.DMA((n_groups, 2)),
            pltpu.SemaphoreType.DMA((2,)),
            pltpu.SemaphoreType.DMA((2,)),
            pltpu.SemaphoreType.DMA((2, 4)),
            pltpu.SemaphoreType.DMA,
            pltpu.SemaphoreType.DMA,
        ],
        compiler_params=pltpu.CompilerParams(collective_id=0, has_side_effects=True, vmem_limit_bytes=60 * 2**20),
        name='gather_project',
    )(hidden, seg_ids, w_qkv)


def attention_kernel(tk, scale2, bounds, q_ref, k_ref, v_ref, segq_ref, segk_ref, o_ref, vt, s_even, s_odd, acc):
    i = pl.program_id(1)
    tq, head_dim = q_ref.shape

    @pl.when(i == 0)
    def _():
        vt[...] = v_ref[...].T

    lo, hi = bounds[0, i], bounds[1, i]
    q = q_ref[...]

    def at(chunk):
        return pl.ds(pl.multiple_of(chunk * tk, tk), tk)

    def scores(chunk, s_ref):
        s = lax.dot_general(k_ref[at(chunk), :], q, (((1,), (1,)), ((), ())), preferred_element_type=jnp.float32)
        segk = segk_ref[at(chunk), :]
        allowed = jnp.concatenate([segk] * (tq // segk.shape[1]), axis=1) == segq_ref[:1, :]
        s = jnp.where(allowed, s, -jnp.inf)
        s_ref[...] = s
        return jnp.max(s, axis=0, keepdims=True)

    def absorb(chunk, s, top, m, l):
        m_new = jnp.maximum(m, top)
        p = jnp.exp2((s - m_new) * scale2)
        alpha = jnp.exp2((m - m_new) * scale2)
        l = l * alpha + jnp.sum(p, axis=0, keepdims=True)
        acc[...] = acc[...] * alpha + lax.dot_general(vt[:, at(chunk)], p.astype(jnp.bfloat16), (((1,), (0,)), ((), ())),
                                                      preferred_element_type=jnp.float32)
        return m_new, l

    def pair_step(n, state):
        m, l, top_even = state
        chunk = lo + 2 * n
        top_odd = scores(chunk + 1, s_odd)
        m, l = absorb(chunk, s_even[...], top_even, m, l)
        top_even = scores(jnp.minimum(chunk + 2, hi - 1), s_even)
        m, l = absorb(chunk + 1, s_odd[...], top_odd, m, l)
        return m, l, top_even

    acc[...] = jnp.zeros_like(acc)
    m, l = jnp.full((1, tq), jnp.finfo(jnp.float32).min, jnp.float32), jnp.zeros((1, tq), jnp.float32)
    top = scores(lo, s_even)
    m, l, top = lax.fori_loop(0, (hi - lo) // 2, pair_step, (m, l, top))
    m, l = lax.fori_loop(0, (hi - lo) % 2, lambda n, state: absorb(hi - 1, s_even[...], top, *state), (m, l))
    o_ref[...] = (acc[...] / l).T.astype(o_ref.dtype)


def attention(qkv, seg, heads, head_dim, tq, tk):
    length = qkv.shape[0]
    n_q = length // tq
    first, last = seg[::tq], seg[tq - 1::tq]
    start = jnp.sum(seg[None, :] < first[:, None], axis=1)
    stop = jnp.sum(seg[None, :] <= last[:, None], axis=1)
    bounds = jnp.stack([start // tk, (stop + tk - 1) // tk]).astype(jnp.int32)
    segq = jnp.broadcast_to(seg[None, :], (8, length))
    segk = jnp.broadcast_to(seg[:, None], (length, 128))
    scale2 = head_dim ** -0.5 * math.log2(math.e)
    return pl.pallas_call(
        functools.partial(attention_kernel, tk, scale2),
        out_shape=jax.ShapeDtypeStruct((length, heads * head_dim), jnp.bfloat16),
        grid_spec=pltpu.PrefetchScalarGridSpec(
            num_scalar_prefetch=1, grid=(heads, n_q),
            in_specs=[
                pl.BlockSpec((tq, head_dim), lambda h, i, b: (i, h)),
                pl.BlockSpec((length, head_dim), lambda h, i, b: (0, heads + h)),
                pl.BlockSpec((length, head_dim), lambda h, i, b: (0, 2 * heads + h)),
                pl.BlockSpec((8, tq), lambda h, i, b: (0, i)),
                pl.BlockSpec((length, 128), lambda h, i, b: (0, 0)),
            ],
            out_specs=pl.BlockSpec((tq, head_dim), lambda h, i, b: (i, h)),
            scratch_shapes=[
                pltpu.VMEM((head_dim, length), jnp.bfloat16),
                pltpu.VMEM((tk, tq), jnp.float32),
                pltpu.VMEM((tk, tq), jnp.float32),
                pltpu.VMEM((head_dim, tq), jnp.float32),
            ]),
        compiler_params=pltpu.CompilerParams(vmem_limit_bytes=48 * 2**20),
        name='attention',
    )(bounds, qkv, qkv, qkv, segq, segk)


def solution(mesh):
    n_cp, n_sp = mesh.shape['cp'], mesh.shape['sp']
    n_blocks = n_cp * n_sp
    columns = n_cp // CORES
    token_spec = P('dp', ('cp', 'sp'), None)
    seg_spec = P('dp', ('cp', 'sp'))

    def local_layer(hidden, seg_ids, w_qkv, w_out):
        batch, tokens, depth = hidden.shape
        n_heads, head_dim = w_out.shape[:2]
        groups = n_blocks // batch
        assert n_sp == 4 and columns == 4 and groups == 4 and batch == 2 * columns
        heads = n_heads // groups
        x, core, pair, end = place(lax.axis_index('cp'), lax.axis_index('sp'))
        seq = x * 2 + pair
        qkv, seg = gather_project(hidden, seg_ids, w_qkv, heads, columns, n_blocks)
        seg = lax.dynamic_slice(seg, (0, seq, 0), (n_blocks, 1, tokens)).reshape(n_blocks * tokens)
        o = attention(qkv, seg, heads, head_dim, 512, 512)

        o = o.reshape(n_blocks, tokens, heads * head_dim)
        o = lax.all_to_all(o, ('cp', 'sp'), 0, 0, tiled=True)
        o = o.reshape(columns, CORES, 2, 2, tokens, heads * head_dim)
        o = o.transpose(0, 2, 4, 1, 3, 5).reshape(batch, tokens, n_heads * head_dim)
        y = jnp.dot(o, w_out.reshape(n_heads * head_dim, depth), preferred_element_type=jnp.float32)
        return y.astype(jnp.bfloat16)

    return jax.shard_map(local_layer, mesh=mesh, in_specs=(token_spec, seg_spec, P(), P()), out_specs=token_spec,
                         check_vma=False)
```

time: 738 us -> 480 us (0.65)
  Pallas kernels: 473 us -> 345 us
  blocking collectives: 154 us -> 86.5 us
  local copies, waits for them, and re-layouts: 84 us -> 22 us
    pallas_call x1, Pallas kernels: 254 us -> 183 us  [gather_project(): pl.pallas_call(functools.partial(gather_project_kernel, columns, heads),...]
    pallas_call x1, Pallas kernels: 219 us -> 162 us  [attention(): pl.pallas_call(functools.partial(attention_kernel, tk, scale2), out_shape...]
    all_to_all x1, blocking collectives: 123 us -> 86.5 us  [local_layer(): o = lax.all_to_all(o, ('cp', 'sp'), 0, 0, tiled=True)]
    all_gather x1 -> x0, blocking collectives: 30.3 us -> none  [local_layer(): seg = lax.all_gather(seg_ids, ('cp', 'sp'), axis=1, tiled=True)]
    unnamed x1 -> x0, local copies, waits for them, and re-layouts: 22.6 us -> none
    dynamic_slice x2 -> x1, local copies, waits for them, and re-layouts: 22.6 us -> 0.93 us  [local_layer(): lax.dynamic_slice(seg, (0, seq, 0), (n_blocks, 1, tokens))]
    reshape x1 -> x0, local copies, waits for them, and re-layouts: 17.8 us -> none  [local_layer(): w_local = w_local.reshape(depth, 3 * heads * head_dim)]
where the time goes in v2:
time: 480 us; the launch traced here: 479 us
  Pallas kernels  345 us (72%)
  blocking collectives  86.5 us (18%)
  matrix products  25.5 us (5%)
  local copies, waits for them, and re-layouts  22 us (5%)
    pallas_call x1, Pallas kernels, gather_project(): pl.pallas_call(functools.partial(gather_project_kernel, columns, heads),...  183 us
    pallas_call x1, Pallas kernels, attention(): pl.pallas_call(functools.partial(attention_kernel, tk, scale2), out_shape...  162 us
    all_to_all x1, blocking collectives, local_layer(): o = lax.all_to_all(o, ('cp', 'sp'), 0, 0, tiled=True)  86.5 us
    dot_general x1, matrix products, local_layer(): jnp.dot(o, w_out.reshape(n_heads * head_dim, depth), preferred_element_ty...  25.5 us
    reshape x1, local copies, waits for them, and re-layouts, local_layer(): o = o.transpose(0, 2, 4, 1, 3, 5).reshape(batch, tokens, n_heads * head_dim)  14.4 us

profile of v2, /device:TPU:99, one launch (start us, length us, event | category | flops | bytes accessed | tf_op | source)
XLA Modules:
  0.0 479.4 jit_solution(2142385044575551549)
XLA Ops:
  0.0 183.3 %gather_project.1 = (bf16[4096,2304]{1,0:T(8,128)(2,1)}, s32[32,8,128]{2,1,0:T(8,128)}) custom-call(bf16[8,128,3072]{2,1,0:T(8,128)(2,1)} %hid.1, s32[8,128]{1,0:T(8,128)} %seg.1, bf16[3072,3,24,128]{3,2,1,0:T(8,128)(2,1)} %w_hbm.1), custom_call_target="tpu_custom_call" | custom-call | tf_op jit(solution)/shard_map/gather_project/pallas_call | solution.py:218
  183.3 0.9 constant_dynamic-slice_fusion
  184.3 0.1 slice.7
  184.4 0.1 slice.6
  184.4 0.3 convert_reduce_fusion.1
  184.8 0.6 broadcast_in_dim.2.segk_ref
  185.4 161.6 %attention.1 = bf16[4096,768]{1,0:T(8,128)(2,1)} custom-call(s32[2,8]{1,0:T(2,128)S(1)} %pad_add_fusion.bounds, bf16[4096,2304]{1,0:T(8,128)(2,1)} %get-tuple-element.8.q_ref.k_ref.v_ref, bf16[4096,2304]{1,0:T(8,128)(2,1)} %get-tuple-element.8.q_ref.k_ref.v_ref, bf16[4096,2304]{1,0:T(8,128)(2,1)} %get-tuple-element.8.q_ref.k_ref.v_ref, ...), custom_call_target="tpu_custom_call" | custom-call | tf_op jit(solution)/shard_map/attention/pallas_call | solution.py:303
  347.0 86.5 %all_to_all.5 = bf16[32,128,768]{2,1,0:T(8,128)(2,1)S(1)} all-to-all(bf16[32,128,768]{2,1,0:T(8,128)(2,1)} %bitcast.27), channel_id=1, replica_groups=mesh['dp'=1,'sp'=4,'cp'=8] {'cp','sp'}, dimensions={0} | all-to-all | bytes 12582912 | tf_op jit(solution)/shard_map/all_to_all | solution.py:347
  433.5 5.9 %copy.7 = bf16[4,2,2,2,128,768]{5,3,1,4,2,0:T(2,128)(2,1)} copy(bf16[4,2,2,2,128,768]{5,4,3,2,1,0:T(8,128)(2,1)S(1)} %bitcast.28) | data formatting | bytes 12582912 | tf_op jit(solution)/shard_map/reshape | solution.py:348
  439.4 14.4 %reshape.122 = bf16[8,128,3072]{2,1,0:T(8,128)(2,1)} reshape(bf16[4,2,128,2,2,768]{5,4,3,2,1,0:T(2,128)(2,1)} %bitcast.29) | data formatting | bytes 12582912 | tf_op jit(solution)/shard_map/reshape | solution.py:349
  453.8 25.5 %convolution_convert_fusion = bf16[8,128,3072]{2,1,0:T(8,128)(2,1)} fusion(bf16[8,128,3072]{2,1,0:T(8,128)(2,1)} %reshape.122, bf16[3072,3072,1]{1,0,2:T(8,128)(2,1)} %bitcast.35), kind=kOutput, calls=%fused_computation.1 | convolution fusion | flops 19330498560 | bytes 31457280 | tf_op jit(solution)/shard_map/dot_general | solution.py:350
  (3 shorter events, 0.0 us)

commit v3 on v2

--- a/solution.py
+++ b/solution.py
@@ -10,6 +10,7 @@
 
 MESH = pl.DeviceIdType.MESH
 CORES = 2
+VMEM_LIMIT = 67043328
 
 
 def place(rank, lane):
@@ -237,7 +238,7 @@
             pltpu.SemaphoreType.DMA,
             pltpu.SemaphoreType.DMA,
         ],
-        compiler_params=pltpu.CompilerParams(collective_id=0, has_side_effects=True, vmem_limit_bytes=60 * 2**20),
+        compiler_params=pltpu.CompilerParams(collective_id=0, has_side_effects=True, vmem_limit_bytes=VMEM_LIMIT),
         name='gather_project',
     )(hidden, seg_ids, w_qkv)
 
@@ -290,7 +291,7 @@
     o_ref[...] = (acc[...] / l).T.astype(o_ref.dtype)
 
 
-def attention(qkv, seg, heads, head_dim, tq, tk):
+def attention(qkv, seg, heads, head_dim, tq, tk, h0, nh):
     length = qkv.shape[0]
     n_q = length // tq
     first, last = seg[::tq], seg[tq - 1::tq]
@@ -302,13 +303,13 @@
     scale2 = head_dim ** -0.5 * math.log2(math.e)
     return pl.pallas_call(
         functools.partial(attention_kernel, tk, scale2),
-        out_shape=jax.ShapeDtypeStruct((length, heads * head_dim), jnp.bfloat16),
+        out_shape=jax.ShapeDtypeStruct((length, nh * head_dim), jnp.bfloat16),
         grid_spec=pltpu.PrefetchScalarGridSpec(
-            num_scalar_prefetch=1, grid=(heads, n_q),
+            num_scalar_prefetch=1, grid=(nh, n_q),
             in_specs=[
-                pl.BlockSpec((tq, head_dim), lambda h, i, b: (i, h)),
-                pl.BlockSpec((length, head_dim), lambda h, i, b: (0, heads + h)),
-                pl.BlockSpec((length, head_dim), lambda h, i, b: (0, 2 * heads + h)),
+                pl.BlockSpec((tq, head_dim), lambda h, i, b: (i, h0 + h)),
+                pl.BlockSpec((length, head_dim), lambda h, i, b: (0, heads + h0 + h)),
+                pl.BlockSpec((length, head_dim), lambda h, i, b: (0, 2 * heads + h0 + h)),
                 pl.BlockSpec((8, tq), lambda h, i, b: (0, i)),
                 pl.BlockSpec((length, 128), lambda h, i, b: (0, 0)),
             ],
@@ -319,9 +320,68 @@
                 pltpu.VMEM((tk, tq), jnp.float32),
                 pltpu.VMEM((head_dim, tq), jnp.float32),
             ]),
-        compiler_params=pltpu.CompilerParams(vmem_limit_bytes=48 * 2**20),
+        compiler_params=pltpu.CompilerParams(vmem_limit_bytes=VMEM_LIMIT),
+        cost_estimate=pl.CostEstimate(flops=4 * nh * length * length * head_dim, transcendentals=0,
+                                      bytes_accessed=8 * nh * length * head_dim),
         name='attention',
     )(bounds, qkv, qkv, qkv, segq, segk)
+
+
+def out_kernel(columns, heads, parts, has_acc, *refs):
+    n = len(parts)
+    o_refs, w_ref, refs = refs[:n], refs[n], refs[n + 1:]
+    acc_ref, refs = (refs[0], refs[1:]) if has_acc else (None, refs)
+    y_ref, lhs, sem = refs
+    batch, tokens = lhs.shape[:2]
+
+    @pl.when(pl.program_id(0) == 0)
+    def _():
+        copies = []
+        for seq in range(batch):
+            at = 0
+            for group in range(4):
+                source = (seq // 2) * 8 + (group // 2) * 4 + (seq % 2) * 2 + group % 2
+                for k in range(n):
+                    size = o_refs[k].shape[2]
+                    copies.append(pltpu.make_async_copy(o_refs[k].at[source], lhs.at[seq, :, pl.ds(at, size)], sem))
+                    at += size
+        for copy in copies:
+            copy.start()
+        for copy in copies:
+            copy.wait()
+
+    depth = lhs.shape[2]
+    y = jnp.dot(lhs[...].reshape(batch * tokens, depth), w_ref[...].reshape(depth, w_ref.shape[-1]),
+                preferred_element_type=jnp.float32)
+    y = y.reshape(y_ref.shape)
+    if has_acc:
+        y = acc_ref[...] + y
+    y_ref[...] = y.astype(y_ref.dtype)
+
+
+def out_project(os, starts, w_out, acc, columns, heads, dtype, tile=256):
+    n_heads, head_dim, width = w_out.shape
+    n_blocks, tokens, _ = os[0].shape
+    groups = n_heads // heads
+    batch = n_blocks // groups
+    count = sum(o.shape[2] for o in os) // head_dim
+    first = starts[0]
+    w = w_out.reshape(groups, heads, head_dim, width)
+    w_spec = pl.BlockSpec(tuple(pl.Element(n) for n in (groups, count, head_dim, tile)), lambda i: (0, first, 0, i * tile))
+    y_spec = pl.BlockSpec((batch, tokens, tile), lambda i: (0, 0, i))
+    ins = [*os, w] + ([] if acc is None else [acc])
+    return pl.pallas_call(
+        functools.partial(out_kernel, columns, heads, starts, acc is not None),
+        out_shape=jax.ShapeDtypeStruct((batch, tokens, width), dtype),
+        grid=(width // tile,),
+        in_specs=[pl.BlockSpec(memory_space=pl.ANY)] * len(os) + [w_spec] + ([] if acc is None else [y_spec]),
+        out_specs=y_spec,
+        scratch_shapes=[pltpu.VMEM((batch, tokens, groups * count * head_dim), jnp.bfloat16), pltpu.SemaphoreType.DMA],
+        compiler_params=pltpu.CompilerParams(vmem_limit_bytes=VMEM_LIMIT),
+        cost_estimate=pl.CostEstimate(flops=2 * batch * tokens * groups * count * head_dim * width, transcendentals=0,
+                                      bytes_accessed=2 * groups * count * head_dim * width),
+        name='out_project',
+    )(*ins)
 
 
 def solution(mesh):
@@ -341,14 +401,15 @@
         seq = x * 2 + pair
         qkv, seg = gather_project(hidden, seg_ids, w_qkv, heads, columns, n_blocks)
         seg = lax.dynamic_slice(seg, (0, seq, 0), (n_blocks, 1, tokens)).reshape(n_blocks * tokens)
-        o = attention(qkv, seg, heads, head_dim, 512, 512)
-
-        o = o.reshape(n_blocks, tokens, heads * head_dim)
-        o = lax.all_to_all(o, ('cp', 'sp'), 0, 0, tiled=True)
-        o = o.reshape(columns, CORES, 2, 2, tokens, heads * head_dim)
-        o = o.transpose(0, 2, 4, 1, 3, 5).reshape(batch, tokens, n_heads * head_dim)
-        y = jnp.dot(o, w_out.reshape(n_heads * head_dim, depth), preferred_element_type=jnp.float32)
-        return y.astype(jnp.bfloat16)
+        parts = ((0, heads // 3), (heads // 3, heads // 2), (heads - heads // 6, heads // 6))
+        os = []
+        for h0, nh in parts:
+            o = attention(qkv, seg, heads, head_dim, 512, 512, h0, nh)
+            o = o.reshape(n_blocks, tokens, nh * head_dim)
+            os.append(lax.all_to_all(o, ('cp', 'sp'), 0, 0, tiled=True))
+        starts = [h0 for h0, _ in parts]
+        acc = out_project(os[:-1], starts[:-1], w_out, None, columns, heads, jnp.float32)
+        return out_project(os[-1:], starts[-1:], w_out, acc, columns, heads, jnp.bfloat16)
 
     return jax.shard_map(local_layer, mesh=mesh, in_specs=(token_spec, seg_spec, P(), P()), out_specs=token_spec,
                          check_vma=False)

time: 480 us -> 428 us (0.89)
  blocking collectives: 86.5 us -> 0 us
  Pallas kernels: 345 us -> 390 us
  matrix products: 25.5 us -> 0 us
  starting transfers between devices: 0 us -> 20.3 us
  local copies, waits for them, and re-layouts: 22 us -> 4.73 us
  waiting for transfers between devices: 0 us -> 9.57 us
    all_to_all x1 -> x0, blocking collectives: 86.5 us -> none  [local_layer(): o = lax.all_to_all(o, ('cp', 'sp'), 0, 0, tiled=True)]
    pallas_call x0 -> x2, Pallas kernels: none -> 39.5 us  [out_project(): pl.pallas_call(functools.partial(out_kernel, columns, heads, starts, acc...]
    dot_general x1 -> x0, matrix products: 25.5 us -> none  [local_layer(): jnp.dot(o, w_out.reshape(n_heads * head_dim, depth), preferred_element_ty...]
    reshape x2 -> x0, local copies, waits for them, and re-layouts: 20.3 us -> none  [the longest x1 14.4 us: local_layer(): o = o.transpose(0, 2, 4, 1, 3, 5).reshape(batch, tokens, n_heads * head_dim)]
    all_to_all x0 -> x3, starting transfers between devices: none -> 20.3 us  [local_layer(): os.append(lax.all_to_all(o, ('cp', 'sp'), 0, 0, tiled=True))]
    all_to_all x0 -> x3, waiting for transfers between devices: none -> 9.57 us  [local_layer(): os.append(lax.all_to_all(o, ('cp', 'sp'), 0, 0, tiled=True))]
    pallas_call x1 -> x3, Pallas kernels: 162 us -> 167 us  [attention(): pl.pallas_call(functools.partial(attention_kernel, tk, scale2), out_shape...]
  transfers between devices with their start and end apart: 0 -> 3, of which waited for: 0 -> 1; matrix products, arithmetic and copies ran while one was open for 0% -> 0% of each run, Pallas kernels for 0% -> 32%
where the time goes in v3:
time: 428 us; the launch traced here: 426 us
  Pallas kernels  390 us (91%)
  starting transfers between devices  20.3 us (5%)
  waiting for transfers between devices  9.57 us (2%)
  local copies, waits for them, and re-layouts  4.73 us (1%)
    pallas_call x1, Pallas kernels, gather_project(): pl.pallas_call(functools.partial(gather_project_kernel, columns, heads),...  183 us
    pallas_call x3, Pallas kernels, attention(): pl.pallas_call(functools.partial(attention_kernel, tk, scale2), out_shape...  167 us
    pallas_call x2, Pallas kernels, out_project(): pl.pallas_call(functools.partial(out_kernel, columns, heads, starts, acc...  39.5 us
    all_to_all x3, starting transfers between devices, local_layer(): os.append(lax.all_to_all(o, ('cp', 'sp'), 0, 0, tiled=True))  20.3 us
    all_to_all x3, waiting for transfers between devices, local_layer(): os.append(lax.all_to_all(o, ('cp', 'sp'), 0, 0, tiled=True))  9.57 us
  transfers between devices with their start and end apart: 3, of which 1 were waited for; matrix products, arithmetic and copies ran while one was open for 0% of the time, Pallas kernels for 32%

profile of v3, /device:TPU:99, one launch (start us, length us, event | category | flops | bytes accessed | tf_op | source)
XLA Modules:
  0.0 425.6 jit_solution(7806846639412632973)
XLA Ops:
  0.0 183.3 %gather_project.1 = (bf16[4096,2304]{1,0:T(8,128)(2,1)}, s32[32,8,128]{2,1,0:T(8,128)}) custom-call(bf16[8,128,3072]{2,1,0:T(8,128)(2,1)} %hid.1, s32[8,128]{1,0:T(8,128)} %seg.1, bf16[3072,3,24,128]{3,2,1,0:T(8,128)(2,1)} %w_hbm.1), custom_call_target="tpu_custom_call" | custom-call | tf_op jit(solution)/shard_map/gather_project/pallas_call | solution.py:219
  183.3 0.9 constant_dynamic-slice_fusion
  184.2 0.1 slice.5
  184.3 0.1 slice.4
  184.4 0.3 convert_reduce_fusion.1
  184.7 0.5 pad_add_fusion.bounds
  185.2 0.7 lt.12.segq_ref
  185.9 3.0 broadcast_in_dim.2.segk_ref
  188.9 56.0 %attention.4 = bf16[4096,256]{1,0:T(8,128)(2,1)} custom-call(s32[2,8]{1,0:T(2,128)} %pad_add_fusion.bounds, bf16[4096,2304]{1,0:T(8,128)(2,1)} %get-tuple-element.8.q_ref.k_ref.v_ref, bf16[4096,2304]{1,0:T(8,128)(2,1)} %get-tuple-element.8.q_ref.k_ref.v_ref, bf16[4096,2304]{1,0:T(8,128)(2,1)} %get-tuple-element.8.q_ref.k_ref.v_ref, s32[8,4096]{1,0:T(8,128)} %lt.12.segq_ref, ...), custom_call_target="tpu_custom_call" | custom-call | flops 17179869184 | bytes 8388608 | tf_op jit(solution)/shard_map/attention/pallas_call | solution.py:304
  244.8 6.8 %all-to-all-start.1 = ((bf16[32,128,256]{2,1,0:T(8,128)(2,1)}), bf16[32,128,256]{2,1,0:T(8,128)(2,1)}, u32[]{:S(2)}, u32[]{:S(2)}) async-start(bf16[32,128,256]{2,1,0:T(8,128)(2,1)} %bitcast.25), calls=%async_computation.1 | async-start | bytes 4194304 | tf_op jit(solution)/shard_map/all_to_all | solution.py:409
  251.6 82.4 %attention.5 = bf16[4096,384]{1,0:T(8,128)(2,1)} custom-call(s32[2,8]{1,0:T(2,128)} %pad_add_fusion.bounds, bf16[4096,2304]{1,0:T(8,128)(2,1)} %get-tuple-element.8.q_ref.k_ref.v_ref, bf16[4096,2304]{1,0:T(8,128)(2,1)} %get-tuple-element.8.q_ref.k_ref.v_ref, bf16[4096,2304]{1,0:T(8,128)(2,1)} %get-tuple-element.8.q_ref.k_ref.v_ref, s32[8,4096]{1,0:T(8,128)} %lt.12.segq_ref, ...), custom_call_target="tpu_custom_call" | custom-call | flops 25769803776 | bytes 12582912 | tf_op jit(solution)/shard_map/attention/pallas_call | solution.py:304
  334.0 0.0 all-to-all-done.1.refs_0_
  334.0 4.8 %all-to-all-start.2 = ((bf16[32,128,384]{2,1,0:T(8,128)(2,1)}), bf16[32,128,384]{2,1,0:T(8,128)(2,1)}, u32[]{:S(2)}, u32[]{:S(2)}) async-start(bf16[32,128,384]{2,1,0:T(8,128)(2,1)} %bitcast.24), calls=%async_computation.2 | async-start | bytes 6291456 | tf_op jit(solution)/shard_map/all_to_all | solution.py:409
  338.8 29.0 %attention.3 = bf16[4096,128]{1,0:T(8,128)(2,1)} custom-call(s32[2,8]{1,0:T(2,128)} %pad_add_fusion.bounds, bf16[4096,2304]{1,0:T(8,128)(2,1)} %get-tuple-element.8.q_ref.k_ref.v_ref, bf16[4096,2304]{1,0:T(8,128)(2,1)} %get-tuple-element.8.q_ref.k_ref.v_ref, bf16[4096,2304]{1,0:T(8,128)(2,1)} %get-tuple-element.8.q_ref.k_ref.v_ref, s32[8,4096]{1,0:T(8,128)} %lt.12.segq_ref, ...), custom_call_target="tpu_custom_call" | custom-call | flops 8589934592 | bytes 4194304 | tf_op jit(solution)/shard_map/attention/pallas_call | solution.py:304
  367.8 9.6 %all-to-all-done.2.refs_1_ = bf16[32,128,384]{2,1,0:T(8,128)(2,1)} async-done(((bf16[32,128,384]{2,1,0:T(8,128)(2,1)}), bf16[32,128,384]{2,1,0:T(8,128)(2,1)}, u32[]{:S(2)}, u32[]{:S(2)}) %all-to-all-start.2) | async-done | bytes 3145760 | tf_op jit(solution)/shard_map/all_to_all | solution.py:409
  377.4 8.7 %all-to-all-start = ((bf16[32,128,128]{2,1,0:T(8,128)(2,1)}), bf16[32,128,128]{2,1,0:T(8,128)(2,1)}, u32[]{:S(2)}, u32[]{:S(2)}) async-start(bf16[32,128,128]{2,1,0:T(8,128)(2,1)} %bitcast.23), calls=%async_computation | async-start | bytes 2097152 | tf_op jit(solution)/shard_map/all_to_all | solution.py:409
  386.0 24.5 %out_project.2.refs_2_ = f32[8,128,3072]{2,1,0:T(8,128)} custom-call(bf16[32,128,256]{2,1,0:T(8,128)(2,1)} %all-to-all-done.1.refs_0_, bf16[32,128,384]{2,1,0:T(8,128)(2,1)} %all-to-all-done.2.refs_1_, bf16[4,6,128,3072]{3,2,1,0:T(8,128)(2,1)} %bitcast.21), custom_call_target="tpu_custom_call" | custom-call | flops 16106127360 | bytes 15728640 | tf_op jit(solution)/shard_map/out_project/pallas_call | solution.py:373
  410.5 0.0 all-to-all-done.refs_0_
  410.6 15.0 %out_project.3 = bf16[8,128,3072]{2,1,0:T(8,128)(2,1)} custom-call(bf16[32,128,128]{2,1,0:T(8,128)(2,1)} %all-to-all-done.refs_0_, bf16[4,6,128,3072]{3,2,1,0:T(8,128)(2,1)} %bitcast.22, f32[8,128,3072]{2,1,0:T(8,128)} %out_project.2.refs_2_), custom_call_target="tpu_custom_call" | custom-call | flops 3221225472 | bytes 3145728 | tf_op jit(solution)/shard_map/out_project/pallas_call | solution.py:373
  (1 shorter events, 0.0 us)
Async XLA Ops:
  244.8 89.2 %all-to-all-start.1 = ((bf16[32,128,256]{2,1,0:T(8,128)(2,1)}), bf16[32,128,256]{2,1,0:T(8,128)(2,1)}, u32[]{:S(2)}, u32[]{:S(2)}) async-start(bf16[32,128,256]{2,1,0:T(8,128)(2,1)} %bitcast.25), calls=%async_computation.1 | async-start | bytes 4194304 | tf_op jit(solution)/shard_map/all_to_all | solution.py:409
  334.0 43.4 %all-to-all-start.2 = ((bf16[32,128,384]{2,1,0:T(8,128)(2,1)}), bf16[32,128,384]{2,1,0:T(8,128)(2,1)}, u32[]{:S(2)}, u32[]{:S(2)}) async-start(bf16[32,128,384]{2,1,0:T(8,128)(2,1)} %bitcast.24), calls=%async_computation.2 | async-start | bytes 6291456 | tf_op jit(solution)/shard_map/all_to_all | solution.py:409
  377.4 33.2 %all-to-all-start = ((bf16[32,128,128]{2,1,0:T(8,128)(2,1)}), bf16[32,128,128]{2,1,0:T(8,128)(2,1)}, u32[]{:S(2)}, u32[]{:S(2)}) async-start(bf16[32,128,128]{2,1,0:T(8,128)(2,1)} %bitcast.23), calls=%async_computation | async-start | bytes 2097152 | tf_op jit(solution)/shard_map/all_to_all | solution.py:409

commit v4 on v3

--- a/solution.py
+++ b/solution.py
@@ -18,7 +18,8 @@
 
 
 def gather_project_kernel(columns, heads, hid, seg, w_hbm, out, seg_out, blocks, w_vmem, stage, w_in, w_wide, recv_sem,
-                          direct_sem, relay_sem, twin_sem, w_sem, own_sem, out_sem, seg_send, seg_recv):
+                          direct_sem, relay_sem, twin_sem, w_sem, own_sem, out_sem, seg_send, seg_recv, transit, transit_recv,
+                          transit_send):
     rank, lane = lax.axis_index('cp'), lax.axis_index('sp')
     x, core, pair, end = place(rank, lane)
     far = 3 - lane
@@ -33,8 +34,7 @@
         return ((xx * 2 + hh) * CORES + cc) * 2 + ee
 
     me = slot_of(x, pair, core, end)
-    steps = [(dx, other) for dx in (0, 1, columns - 1, 2) for other in (0, 1)]
-    n_groups = len(steps)
+    n_groups = n_blocks // 4
     twin = dev(x, 1 - core, lane)
     partner = dev(x, core, mate)
 
@@ -70,14 +70,30 @@
     w_copy(0).start()
     pl.semaphore_wait(barrier, n_blocks - 1)
 
+    right, left = (x + 1) % columns, (x + columns - 1) % columns
+    across = (x + 2) % columns
     directs = []
-    for i, (dx, other) in enumerate(steps[1:]):
-        xt = (x + columns - dx) % columns
-        copy = pltpu.make_async_remote_copy(
-            src_ref=hid.at[xt * 2 + (1 - pair if other else pair)], dst_ref=blocks.at[me], send_sem=direct_sem.at[i],
-            recv_sem=recv_sem.at[me], device_id=dev(xt, core, far if other else lane), device_id_type=MESH)
+    sends = [(across * 2 + pair, transit.at[0], transit_recv.at[0], dev(right, core, lane)),
+             (across * 2 + 1 - pair, transit.at[1], transit_recv.at[1], dev(left, core, lane))]
+    for xt, other in ((x, 1), (left, 0), (right, 0), (left, 1), (right, 1)):
+        sends.append((xt * 2 + (1 - pair if other else pair), blocks.at[me], recv_sem.at[me],
+                      dev(xt, core, far if other else lane)))
+    for i, (seq, place_, sem, device) in enumerate(sends):
+        copy = pltpu.make_async_remote_copy(src_ref=hid.at[seq], dst_ref=place_, send_sem=direct_sem.at[i], recv_sem=sem,
+                                            device_id=device, device_id_type=MESH)
         copy.start()
         directs.append(copy)
+
+    passes = [
+        pltpu.make_async_remote_copy(
+            src_ref=transit.at[0], dst_ref=blocks.at[slot_of(left, pair, core, end)], send_sem=transit_send.at[0],
+            recv_sem=recv_sem.at[slot_of(left, pair, core, end)], device_id=dev(right, core, lane), device_id_type=MESH),
+        pltpu.make_async_remote_copy(
+            src_ref=transit.at[1], dst_ref=blocks.at[slot_of(right, pair, core, end)], send_sem=transit_send.at[1],
+            recv_sem=recv_sem.at[slot_of(right, pair, core, end)], device_id=dev(left, core, far), device_id_type=MESH)]
+    arrivals = [pltpu.make_async_remote_copy(
+        src_ref=transit.at[n], dst_ref=transit.at[n], send_sem=transit_send.at[n], recv_sem=transit_recv.at[n],
+        device_id=twin, device_id_type=MESH) for n in range(2)]
 
     def remote(slot, sem, device):
         return pltpu.make_async_remote_copy(
@@ -139,6 +155,9 @@
     lax.fori_loop(0, n_chunks // 2, relay_weights, 0)
     serve(1)
     lax.fori_loop(n_chunks // 2, n_chunks, relay_weights, 0)
+    for arrival, copy in zip(arrivals, passes):
+        arrival.wait_recv()
+        copy.start()
 
     rows = stage.shape[1] // 4
     tile = 256
@@ -186,7 +205,7 @@
 
     lax.fori_loop(0, n_groups, step, 0)
 
-    for copy in directs:
+    for copy in directs + passes:
         copy.wait_send()
 
     def drain(j, carry):
@@ -237,6 +256,9 @@
             pltpu.SemaphoreType.DMA((2, 4)),
             pltpu.SemaphoreType.DMA,
             pltpu.SemaphoreType.DMA,
+            pltpu.VMEM((2, tokens, depth), jnp.bfloat16),
+            pltpu.SemaphoreType.DMA((2,)),
+            pltpu.SemaphoreType.DMA((2,)),
         ],
         compiler_params=pltpu.CompilerParams(collective_id=0, has_side_effects=True, vmem_limit_bytes=VMEM_LIMIT),
         name='gather_project',
@@ -359,8 +381,9 @@
     y_ref[...] = y.astype(y_ref.dtype)
 
 
-def out_project(os, starts, w_out, acc, columns, heads, dtype, tile=256):
+def out_project(os, starts, w_out, acc, columns, heads, dtype, tile=512):
     n_heads, head_dim, width = w_out.shape
+    tile = min(tile, width)
     n_blocks, tokens, _ = os[0].shape
     groups = n_heads // heads
     batch = n_blocks // groups

time: 428 us -> 414 us (0.967)
  Pallas kernels: 390 us -> 377 us
    pallas_call x1, Pallas kernels: 183 us -> 174 us  [gather_project(): pl.pallas_call(functools.partial(gather_project_kernel, columns, heads),...]
    pallas_call x2, Pallas kernels: 39.5 us -> 35.1 us  [out_project(): pl.pallas_call(functools.partial(out_kernel, columns, heads, starts, acc...]
  transfers between devices with their start and end apart: 3 -> 3, of which waited for: 1 -> 1; matrix products, arithmetic and copies ran while one was open for 0% -> 0% of each run, Pallas kernels for 32% -> 33%
where the time goes in v4:
time: 414 us; the launch traced here: 413 us
  Pallas kernels  377 us (91%)
  starting transfers between devices  21 us (5%)
  waiting for transfers between devices  9.56 us (2%)
  local copies, waits for them, and re-layouts  4.73 us (1%)
    pallas_call x1, Pallas kernels, gather_project(): pl.pallas_call(functools.partial(gather_project_kernel, columns, heads),...  174 us
    pallas_call x3, Pallas kernels, attention(): pl.pallas_call(functools.partial(attention_kernel, tk, scale2), out_shape...  167 us
    pallas_call x2, Pallas kernels, out_project(): pl.pallas_call(functools.partial(out_kernel, columns, heads, starts, acc...  35.1 us
    all_to_all x3, starting transfers between devices, local_layer(): os.append(lax.all_to_all(o, ('cp', 'sp'), 0, 0, tiled=True))  21 us
    all_to_all x3, waiting for transfers between devices, local_layer(): os.append(lax.all_to_all(o, ('cp', 'sp'), 0, 0, tiled=True))  9.56 us
  transfers between devices with their start and end apart: 3, of which 1 were waited for; matrix products, arithmetic and copies ran while one was open for 0% of the time, Pallas kernels for 33%

profile of v4, /device:TPU:99, one launch (start us, length us, event | category | flops | bytes accessed | tf_op | source)
XLA Modules:
  0.0 412.9 jit_solution(12465046032957465225)
XLA Ops:
  0.0 174.2 %gather_project.1 = (bf16[4096,2304]{1,0:T(8,128)(2,1)}, s32[32,8,128]{2,1,0:T(8,128)}) custom-call(bf16[8,128,3072]{2,1,0:T(8,128)(2,1)} %hid.1, s32[8,128]{1,0:T(8,128)} %seg.1, bf16[3072,3,24,128]{3,2,1,0:T(8,128)(2,1)} %w_hbm.1), custom_call_target="tpu_custom_call" | custom-call | tf_op jit(solution)/shard_map/gather_project/pallas_call | solution.py:238
  174.3 0.9 constant_dynamic-slice_fusion
  175.2 0.1 slice.5
  175.3 0.1 slice.4
  175.4 0.3 convert_reduce_fusion.1
  175.6 0.5 pad_add_fusion.bounds
  176.2 0.7 lt.12.segq_ref
  176.8 3.0 broadcast_in_dim.2.segk_ref
  179.8 56.0 %attention.4 = bf16[4096,256]{1,0:T(8,128)(2,1)} custom-call(s32[2,8]{1,0:T(2,128)} %pad_add_fusion.bounds, bf16[4096,2304]{1,0:T(8,128)(2,1)} %get-tuple-element.8.q_ref.k_ref.v_ref, bf16[4096,2304]{1,0:T(8,128)(2,1)} %get-tuple-element.8.q_ref.k_ref.v_ref, bf16[4096,2304]{1,0:T(8,128)(2,1)} %get-tuple-element.8.q_ref.k_ref.v_ref, s32[8,4096]{1,0:T(8,128)} %lt.12.segq_ref, ...), custom_call_target="tpu_custom_call" | custom-call | flops 17179869184 | bytes 8388608 | tf_op jit(solution)/shard_map/attention/pallas_call | solution.py:326
  235.8 6.3 %all-to-all-start.1 = ((bf16[32,128,256]{2,1,0:T(8,128)(2,1)}), bf16[32,128,256]{2,1,0:T(8,128)(2,1)}, u32[]{:S(2)}, u32[]{:S(2)}) async-start(bf16[32,128,256]{2,1,0:T(8,128)(2,1)} %bitcast.25), calls=%async_computation.1 | async-start | bytes 4194304 | tf_op jit(solution)/shard_map/all_to_all | solution.py:432
  242.0 82.4 %attention.5 = bf16[4096,384]{1,0:T(8,128)(2,1)} custom-call(s32[2,8]{1,0:T(2,128)} %pad_add_fusion.bounds, bf16[4096,2304]{1,0:T(8,128)(2,1)} %get-tuple-element.8.q_ref.k_ref.v_ref, bf16[4096,2304]{1,0:T(8,128)(2,1)} %get-tuple-element.8.q_ref.k_ref.v_ref, bf16[4096,2304]{1,0:T(8,128)(2,1)} %get-tuple-element.8.q_ref.k_ref.v_ref, s32[8,4096]{1,0:T(8,128)} %lt.12.segq_ref, ...), custom_call_target="tpu_custom_call" | custom-call | flops 25769803776 | bytes 12582912 | tf_op jit(solution)/shard_map/attention/pallas_call | solution.py:326
  324.4 0.0 all-to-all-done.1.refs_0_
  324.4 6.1 %all-to-all-start.2 = ((bf16[32,128,384]{2,1,0:T(8,128)(2,1)}), bf16[32,128,384]{2,1,0:T(8,128)(2,1)}, u32[]{:S(2)}, u32[]{:S(2)}) async-start(bf16[32,128,384]{2,1,0:T(8,128)(2,1)} %bitcast.24), calls=%async_computation.2 | async-start | bytes 6291456 | tf_op jit(solution)/shard_map/all_to_all | solution.py:432
  330.5 29.0 %attention.3 = bf16[4096,128]{1,0:T(8,128)(2,1)} custom-call(s32[2,8]{1,0:T(2,128)} %pad_add_fusion.bounds, bf16[4096,2304]{1,0:T(8,128)(2,1)} %get-tuple-element.8.q_ref.k_ref.v_ref, bf16[4096,2304]{1,0:T(8,128)(2,1)} %get-tuple-element.8.q_ref.k_ref.v_ref, bf16[4096,2304]{1,0:T(8,128)(2,1)} %get-tuple-element.8.q_ref.k_ref.v_ref, s32[8,4096]{1,0:T(8,128)} %lt.12.segq_ref, ...), custom_call_target="tpu_custom_call" | custom-call | flops 8589934592 | bytes 4194304 | tf_op jit(solution)/shard_map/attention/pallas_call | solution.py:326
  359.5 9.6 %all-to-all-done.2.refs_1_ = bf16[32,128,384]{2,1,0:T(8,128)(2,1)} async-done(((bf16[32,128,384]{2,1,0:T(8,128)(2,1)}), bf16[32,128,384]{2,1,0:T(8,128)(2,1)}, u32[]{:S(2)}, u32[]{:S(2)}) %all-to-all-start.2) | async-done | bytes 3145760 | tf_op jit(solution)/shard_map/all_to_all | solution.py:432
  369.0 8.7 %all-to-all-start = ((bf16[32,128,128]{2,1,0:T(8,128)(2,1)}), bf16[32,128,128]{2,1,0:T(8,128)(2,1)}, u32[]{:S(2)}, u32[]{:S(2)}) async-start(bf16[32,128,128]{2,1,0:T(8,128)(2,1)} %bitcast.23), calls=%async_computation | async-start | bytes 2097152 | tf_op jit(solution)/shard_map/all_to_all | solution.py:432
  377.7 23.1 %out_project.2.refs_2_ = f32[8,128,3072]{2,1,0:T(8,128)} custom-call(bf16[32,128,256]{2,1,0:T(8,128)(2,1)} %all-to-all-done.1.refs_0_, bf16[32,128,384]{2,1,0:T(8,128)(2,1)} %all-to-all-done.2.refs_1_, bf16[4,6,128,3072]{3,2,1,0:T(8,128)(2,1)} %bitcast.21), custom_call_target="tpu_custom_call" | custom-call | flops 16106127360 | bytes 15728640 | tf_op jit(solution)/shard_map/out_project/pallas_call | solution.py:396
  400.8 0.0 all-to-all-done.refs_0_
  400.8 12.1 %out_project.3 = bf16[8,128,3072]{2,1,0:T(8,128)(2,1)} custom-call(bf16[32,128,128]{2,1,0:T(8,128)(2,1)} %all-to-all-done.refs_0_, bf16[4,6,128,3072]{3,2,1,0:T(8,128)(2,1)} %bitcast.22, f32[8,128,3072]{2,1,0:T(8,128)} %out_project.2.refs_2_), custom_call_target="tpu_custom_call" | custom-call | flops 3221225472 | bytes 3145728 | tf_op jit(solution)/shard_map/out_project/pallas_call | solution.py:396
  (1 shorter events, 0.0 us)
Async XLA Ops:
  235.8 88.7 %all-to-all-start.1 = ((bf16[32,128,256]{2,1,0:T(8,128)(2,1)}), bf16[32,128,256]{2,1,0:T(8,128)(2,1)}, u32[]{:S(2)}, u32[]{:S(2)}) async-start(bf16[32,128,256]{2,1,0:T(8,128)(2,1)} %bitcast.25), calls=%async_computation.1 | async-start | bytes 4194304 | tf_op jit(solution)/shard_map/all_to_all | solution.py:432
  324.4 44.6 %all-to-all-start.2 = ((bf16[32,128,384]{2,1,0:T(8,128)(2,1)}), bf16[32,128,384]{2,1,0:T(8,128)(2,1)}, u32[]{:S(2)}, u32[]{:S(2)}) async-start(bf16[32,128,384]{2,1,0:T(8,128)(2,1)} %bitcast.24), calls=%async_computation.2 | async-start | bytes 6291456 | tf_op jit(solution)/shard_map/all_to_all | solution.py:432
  369.0 31.8 %all-to-all-start = ((bf16[32,128,128]{2,1,0:T(8,128)(2,1)}), bf16[32,128,128]{2,1,0:T(8,128)(2,1)}, u32[]{:S(2)}, u32[]{:S(2)}) async-start(bf16[32,128,128]{2,1,0:T(8,128)(2,1)} %bitcast.23), calls=%async_computation | async-start | bytes 2097152 | tf_op jit(solution)/shard_map/all_to_all | solution.py:432

commit v5 on v4

--- a/solution.py
+++ b/solution.py
@@ -273,17 +273,24 @@
     def _():
         vt[...] = v_ref[...].T
 
-    lo, hi = bounds[0, i], bounds[1, i]
+    lo, full_lo, full_hi, hi = (bounds[n, i] for n in range(4))
     q = q_ref[...]
+    last_chunk = k_ref.shape[0] // tk - 1
+    head = full_lo - lo
+    n_edge, n_full = head + hi - full_hi, full_hi - full_lo
 
     def at(chunk):
         return pl.ds(pl.multiple_of(chunk * tk, tk), tk)
 
-    def scores(chunk, s_ref):
+    def edge(n):
+        return jnp.minimum(jnp.where(n < head, lo + n, full_hi + n - head), last_chunk)
+
+    def scores(chunk, s_ref, masked):
         s = lax.dot_general(k_ref[at(chunk), :], q, (((1,), (1,)), ((), ())), preferred_element_type=jnp.float32)
-        segk = segk_ref[at(chunk), :]
-        allowed = jnp.concatenate([segk] * (tq // segk.shape[1]), axis=1) == segq_ref[:1, :]
-        s = jnp.where(allowed, s, -jnp.inf)
+        if masked:
+            segk = segk_ref[at(chunk), :]
+            allowed = jnp.concatenate([segk] * (tq // segk.shape[1]), axis=1) == segq_ref[:1, :]
+            s = jnp.where(allowed, s, -jnp.inf)
         s_ref[...] = s
         return jnp.max(s, axis=0, keepdims=True)
 
@@ -296,20 +303,27 @@
                                                       preferred_element_type=jnp.float32)
         return m_new, l
 
-    def pair_step(n, state):
-        m, l, top_even = state
-        chunk = lo + 2 * n
-        top_odd = scores(chunk + 1, s_odd)
-        m, l = absorb(chunk, s_even[...], top_even, m, l)
-        top_even = scores(jnp.minimum(chunk + 2, hi - 1), s_even)
-        m, l = absorb(chunk + 1, s_odd[...], top_odd, m, l)
-        return m, l, top_even
+    def run(count, chunk_of, masked, m, l):
+        def pair_step(n, state):
+            m, l, top_even = state
+            n = 2 * n
+            top_odd = scores(chunk_of(n + 1), s_odd, masked)
+            m, l = absorb(chunk_of(n), s_even[...], top_even, m, l)
+            top_even = scores(chunk_of(n + 2), s_even, masked)
+            m, l = absorb(chunk_of(n + 1), s_odd[...], top_odd, m, l)
+            return m, l, top_even
+
+        def odd(n, state):
+            top = scores(chunk_of(0), s_even, masked)
+            m, l, top = lax.fori_loop(0, count // 2, pair_step, (*state, top))
+            return lax.fori_loop(0, count % 2, lambda n, state: absorb(chunk_of(count - 1), s_even[...], top, *state), (m, l))
+
+        return lax.fori_loop(0, jnp.minimum(count, 1), odd, (m, l))
 
     acc[...] = jnp.zeros_like(acc)
     m, l = jnp.full((1, tq), jnp.finfo(jnp.float32).min, jnp.float32), jnp.zeros((1, tq), jnp.float32)
-    top = scores(lo, s_even)
-    m, l, top = lax.fori_loop(0, (hi - lo) // 2, pair_step, (m, l, top))
-    m, l = lax.fori_loop(0, (hi - lo) % 2, lambda n, state: absorb(hi - 1, s_even[...], top, *state), (m, l))
+    m, l = run(n_edge, edge, True, m, l)
+    m, l = run(n_full, lambda n: jnp.minimum(full_lo + n, last_chunk), False, m, l)
     o_ref[...] = (acc[...] / l).T.astype(o_ref.dtype)
 
 
@@ -319,7 +333,10 @@
     first, last = seg[::tq], seg[tq - 1::tq]
     start = jnp.sum(seg[None, :] < first[:, None], axis=1)
     stop = jnp.sum(seg[None, :] <= last[:, None], axis=1)
-    bounds = jnp.stack([start // tk, (stop + tk - 1) // tk]).astype(jnp.int32)
+    lo, hi = start // tk, (stop + tk - 1) // tk
+    full_lo, full_hi = (start + tk - 1) // tk, stop // tk
+    plain = (first == last) & (full_hi > full_lo)
+    bounds = jnp.stack([lo, jnp.where(plain, full_lo, hi), jnp.where(plain, full_hi, hi), hi]).astype(jnp.int32)
     segq = jnp.broadcast_to(seg[None, :], (8, length))
     segk = jnp.broadcast_to(seg[:, None], (length, 128))
     scale2 = head_dim ** -0.5 * math.log2(math.e)
@@ -424,7 +441,7 @@
         seq = x * 2 + pair
         qkv, seg = gather_project(hidden, seg_ids, w_qkv, heads, columns, n_blocks)
         seg = lax.dynamic_slice(seg, (0, seq, 0), (n_blocks, 1, tokens)).reshape(n_blocks * tokens)
-        parts = ((0, heads // 3), (heads // 3, heads // 2), (heads - heads // 6, heads // 6))
+        parts = tuple((n * heads // 3, heads // 3) for n in range(3))
         os = []
         for h0, nh in parts:
             o = attention(qkv, seg, heads, head_dim, 512, 512, h0, nh)

time: 414 us -> 404 us (0.976)
  Pallas kernels: 377 us -> 369 us
    pallas_call x3, Pallas kernels: 167 us -> 161 us  [attention(): pl.pallas_call(functools.partial(attention_kernel, tk, scale2), out_shape...]
  transfers between devices with their start and end apart: 3 -> 3, of which waited for: 1 -> 1; matrix products, arithmetic and copies ran while one was open for 0% -> 0% of each run, Pallas kernels for 33% -> 31%
where the time goes in v5:
time: 404 us; the launch traced here: 403 us
  Pallas kernels  369 us (91%)
  starting transfers between devices  18.3 us (5%)
  waiting for transfers between devices  9.66 us (2%)
  local copies, waits for them, and re-layouts  4.64 us (1%)
    pallas_call x1, Pallas kernels, gather_project(): pl.pallas_call(functools.partial(gather_project_kernel, columns, heads),...  174 us
    pallas_call x3, Pallas kernels, attention(): pl.pallas_call(functools.partial(attention_kernel, tk, scale2), out_shape...  161 us
    pallas_call x2, Pallas kernels, out_project(): pl.pallas_call(functools.partial(out_kernel, columns, heads, starts, acc...  34.1 us
    all_to_all x3, starting transfers between devices, local_layer(): os.append(lax.all_to_all(o, ('cp', 'sp'), 0, 0, tiled=True))  18.3 us
    all_to_all x3, waiting for transfers between devices, local_layer(): os.append(lax.all_to_all(o, ('cp', 'sp'), 0, 0, tiled=True))  9.66 us
  transfers between devices with their start and end apart: 3, of which 1 were waited for; matrix products, arithmetic and copies ran while one was open for 0% of the time, Pallas kernels for 31%

profile of v5, /device:TPU:99, one launch (start us, length us, event | category | flops | bytes accessed | tf_op | source)
XLA Modules:
  0.0 402.7 jit_solution(18167369810357783341)
XLA Ops:
  0.0 174.2 %gather_project.1 = (bf16[4096,2304]{1,0:T(8,128)(2,1)}, s32[32,8,128]{2,1,0:T(8,128)}) custom-call(bf16[8,128,3072]{2,1,0:T(8,128)(2,1)} %hid.1, s32[8,128]{1,0:T(8,128)} %seg.1, bf16[3072,3,24,128]{3,2,1,0:T(8,128)(2,1)} %w_hbm.1), custom_call_target="tpu_custom_call" | custom-call | tf_op jit(solution)/shard_map/gather_project/pallas_call | solution.py:238
  174.2 0.9 constant_dynamic-slice_fusion
  175.2 0.1 slice.5
  175.3 0.1 slice.4
  175.4 0.3 convert_reduce_fusion.1
  175.7 0.5 pad_add_fusion.bounds
  176.2 0.7 lt.12.segq_ref
  176.9 2.9 broadcast_in_dim.2.segk_ref
  179.8 53.7 %attention.5 = bf16[4096,256]{1,0:T(8,128)(2,1)} custom-call(s32[4,8]{1,0:T(4,128)} %pad_add_fusion.bounds, bf16[4096,2304]{1,0:T(8,128)(2,1)} %get-tuple-element.8.q_ref.k_ref.v_ref, bf16[4096,2304]{1,0:T(8,128)(2,1)} %get-tuple-element.8.q_ref.k_ref.v_ref, bf16[4096,2304]{1,0:T(8,128)(2,1)} %get-tuple-element.8.q_ref.k_ref.v_ref, s32[8,4096]{1,0:T(8,128)} %lt.12.segq_ref, ...), custom_call_target="tpu_custom_call" | custom-call | flops 17179869184 | bytes 8388608 | tf_op jit(solution)/shard_map/attention/pallas_call | solution.py:343
  233.4 5.3 %all-to-all-start.2 = ((bf16[32,128,256]{2,1,0:T(8,128)(2,1)}), bf16[32,128,256]{2,1,0:T(8,128)(2,1)}, u32[]{:S(2)}, u32[]{:S(2)}) async-start(bf16[32,128,256]{2,1,0:T(8,128)(2,1)} %bitcast.29), calls=%async_computation.2 | async-start | bytes 4194304 | tf_op jit(solution)/shard_map/all_to_all | solution.py:449
  238.7 53.5 %attention.4 = bf16[4096,256]{1,0:T(8,128)(2,1)} custom-call(s32[4,8]{1,0:T(4,128)} %pad_add_fusion.bounds, bf16[4096,2304]{1,0:T(8,128)(2,1)} %get-tuple-element.8.q_ref.k_ref.v_ref, bf16[4096,2304]{1,0:T(8,128)(2,1)} %get-tuple-element.8.q_ref.k_ref.v_ref, bf16[4096,2304]{1,0:T(8,128)(2,1)} %get-tuple-element.8.q_ref.k_ref.v_ref, s32[8,4096]{1,0:T(8,128)} %lt.12.segq_ref, ...), custom_call_target="tpu_custom_call" | custom-call | flops 17179869184 | bytes 8388608 | tf_op jit(solution)/shard_map/attention/pallas_call | solution.py:343
  292.2 0.0 all-to-all-done.2.refs_1_
  292.2 6.5 %all-to-all-start.1 = ((bf16[32,128,256]{2,1,0:T(8,128)(2,1)}), bf16[32,128,256]{2,1,0:T(8,128)(2,1)}, u32[]{:S(2)}, u32[]{:S(2)}) async-start(bf16[32,128,256]{2,1,0:T(8,128)(2,1)} %bitcast.28), calls=%async_computation.1 | async-start | bytes 4194304 | tf_op jit(solution)/shard_map/all_to_all | solution.py:449
  298.7 53.7 %attention.3 = bf16[4096,256]{1,0:T(8,128)(2,1)} custom-call(s32[4,8]{1,0:T(4,128)} %pad_add_fusion.bounds, bf16[4096,2304]{1,0:T(8,128)(2,1)} %get-tuple-element.8.q_ref.k_ref.v_ref, bf16[4096,2304]{1,0:T(8,128)(2,1)} %get-tuple-element.8.q_ref.k_ref.v_ref, bf16[4096,2304]{1,0:T(8,128)(2,1)} %get-tuple-element.8.q_ref.k_ref.v_ref, s32[8,4096]{1,0:T(8,128)} %lt.12.segq_ref, ...), custom_call_target="tpu_custom_call" | custom-call | flops 17179869184 | bytes 8388608 | tf_op jit(solution)/shard_map/attention/pallas_call | solution.py:343
  352.4 0.0 all-to-all-done.1.refs_0_
  352.4 6.5 %all-to-all-start = ((bf16[32,128,256]{2,1,0:T(8,128)(2,1)}), bf16[32,128,256]{2,1,0:T(8,128)(2,1)}, u32[]{:S(2)}, u32[]{:S(2)}) async-start(bf16[32,128,256]{2,1,0:T(8,128)(2,1)} %bitcast.27), calls=%async_computation | async-start | bytes 4194304 | tf_op jit(solution)/shard_map/all_to_all | solution.py:449
  358.9 19.4 %out_project.2.refs_2_ = f32[8,128,3072]{2,1,0:T(8,128)} custom-call(bf16[32,128,256]{2,1,0:T(8,128)(2,1)} %all-to-all-done.1.refs_0_, bf16[32,128,256]{2,1,0:T(8,128)(2,1)} %all-to-all-done.2.refs_1_, bf16[4,6,128,3072]{3,2,1,0:T(8,128)(2,1)} %bitcast.25), custom_call_target="tpu_custom_call" | custom-call | flops 12884901888 | bytes 12582912 | tf_op jit(solution)/shard_map/out_project/pallas_call | solution.py:413
  378.4 9.7 %all-to-all-done.refs_0_ = bf16[32,128,256]{2,1,0:T(8,128)(2,1)} async-done(((bf16[32,128,256]{2,1,0:T(8,128)(2,1)}), bf16[32,128,256]{2,1,0:T(8,128)(2,1)}, u32[]{:S(2)}, u32[]{:S(2)}) %all-to-all-start) | async-done | bytes 2097184 | tf_op jit(solution)/shard_map/all_to_all | solution.py:449
  388.0 14.6 %out_project.3 = bf16[8,128,3072]{2,1,0:T(8,128)(2,1)} custom-call(bf16[32,128,256]{2,1,0:T(8,128)(2,1)} %all-to-all-done.refs_0_, bf16[4,6,128,3072]{3,2,1,0:T(8,128)(2,1)} %bitcast.26, f32[8,128,3072]{2,1,0:T(8,128)} %out_project.2.refs_2_), custom_call_target="tpu_custom_call" | custom-call | flops 6442450944 | bytes 6291456 | tf_op jit(solution)/shard_map/out_project/pallas_call | solution.py:413
  (3 shorter events, 0.0 us)
Async XLA Ops:
  233.4 58.8 %all-to-all-start.2 = ((bf16[32,128,256]{2,1,0:T(8,128)(2,1)}), bf16[32,128,256]{2,1,0:T(8,128)(2,1)}, u32[]{:S(2)}, u32[]{:S(2)}) async-start(bf16[32,128,256]{2,1,0:T(8,128)(2,1)} %bitcast.29), calls=%async_computation.2 | async-start | bytes 4194304 | tf_op jit(solution)/shard_map/all_to_all | solution.py:449
  292.2 60.2 %all-to-all-start.1 = ((bf16[32,128,256]{2,1,0:T(8,128)(2,1)}), bf16[32,128,256]{2,1,0:T(8,128)(2,1)}, u32[]{:S(2)}, u32[]{:S(2)}) async-start(bf16[32,128,256]{2,1,0:T(8,128)(2,1)} %bitcast.28), calls=%async_computation.1 | async-start | bytes 4194304 | tf_op jit(solution)/shard_map/all_to_all | solution.py:449
  352.4 35.6 %all-to-all-start = ((bf16[32,128,256]{2,1,0:T(8,128)(2,1)}), bf16[32,128,256]{2,1,0:T(8,128)(2,1)}, u32[]{:S(2)}, u32[]{:S(2)}) async-start(bf16[32,128,256]{2,1,0:T(8,128)(2,1)} %bitcast.27), calls=%async_computation | async-start | bytes 4194304 | tf_op jit(solution)/shard_map/all_to_all | solution.py:449
